TPU v7x, 128 devices: a whole 4x4x4 slice. The times are simulated.
128 devices in a mesh: section: 4 (over x_lo, core), tok: 32 (over y, z, x_hi).
Axes of the slice: x: 4 (x_hi: 2, x_lo: 2; x = x_hi * 2 + x_lo), y: 4, z: 4, core: 2. Of those that a mesh axis runs over, the one named last changes fastest.
Arguments:
- states: bfloat16 [8, 2048, 4096], P('section', 'tok'), may hold values from -60 to 60
- spans: int32 [2, 2], replicated, may hold values from 0 to 7, as said below
Outputs:
- bridges: float32 [2, 4096, 4096], P(None, 'section', 'tok')
- residuals: float32 [2, 4096, 4096], P(None, 'section', 'tok')
Inputs may be any that keep to these rules, and one draw needn't show every extreme that they name: `spans`: each row is (start, end) with end - start at least 2.
All inputs are finite; a program needn't handle non-finite values.
Results may differ from a plain program's by a relative error of at most 0.0093.
Values may be sent and summed in bfloat16 or wider, within the bound.
A program may use at most 64 MiB of HBM per device.

v0:
```python
import jax
import jax.numpy as jnp
from jax import lax
from jax.sharding import Mesh
from jax.sharding import PartitionSpec as P

CG_STEPS = 2
SECTION = ("section_0", "section_1")
TOK = ("tok_0", "tok_1", "tok_2")
SECTION_TOK = ("section_0", "section_1", "tok_0", "tok_1", "tok_2")


RIDGE = 0.25


def padded_to(lines, devices):
    spare = -lines.shape[0] % devices
    if not spare:
        return lines
    return jnp.concatenate([lines, jnp.zeros((spare, *lines.shape[1:]), lines.dtype)])


def from_root(value, axis, root):
    lines = jnp.where(lax.axis_index(axis) == root, value, jnp.zeros_like(value)).reshape(
        -1, *value.shape[1:][-1:]
    )
    padded = padded_to(lines, lax.axis_size(axis))
    own = lax.psum_scatter(padded, axis, scatter_dimension=0, tiled=True)
    return lax.all_gather(own, axis, axis=0, tiled=True)[: len(lines)].reshape(value.shape)


def in_blocks(value, dim, devices):
    before, after = (value.shape[:dim], value.shape[dim + 1 :])
    return jnp.moveaxis(value.reshape(*before, devices, -1, *after), dim, 0)


def sum_at_owner(value, axis, dim):
    devices = lax.axis_size(axis)
    blocks = lax.all_to_all(in_blocks(value, dim, devices), axis, 0, 0, tiled=True)
    return jnp.sum(blocks, axis=0)


def joined_along(blocks, dim):
    blocks = jnp.moveaxis(blocks, 0, dim)
    lengths = blocks.shape
    return blocks.reshape(*lengths[:dim], lengths[dim] * lengths[dim + 1], *lengths[dim + 2 :])


def copy_for_each(value, axis):
    copies = jnp.broadcast_to(value, (lax.axis_size(axis), *value.shape))
    return lax.all_to_all(copies, axis, split_axis=0, concat_axis=0, tiled=True)


def gather_directly(value, axis, dim):
    return joined_along(copy_for_each(value, axis), dim)


def over_axes(value, axes):
    for axis in axes:
        value = lax.psum(value, axis)
    return value


def transposed(left, right_hand):
    return lax.dot_general(
        left, right_hand, (((0,), (0,)), ((), ())), preferred_element_type=jnp.float32
    )


def conjugate(operators, rights, summed):
    bridges = [jnp.zeros_like(right_side) for right_side in rights]
    residuals = list(rights)
    directions = list(rights)
    squares = summed([jnp.sum(right_side * right_side) for right_side in rights])
    for step in range(CG_STEPS):
        images = [operators[k](directions[k]) for k in range(len(rights))]
        curvatures = summed([jnp.sum(directions[k] * images[k]) for k in range(len(rights))])
        for k in range(len(rights)):
            step_size = squares[k] / curvatures[k]
            bridges[k] = bridges[k] + step_size * directions[k]
            residuals[k] = residuals[k] - step_size * images[k]
        if step + 1 < CG_STEPS:
            renewed = summed([jnp.sum(residual * residual) for residual in residuals])
            for k in range(len(rights)):
                directions[k] = residuals[k] + renewed[k] / squares[k] * directions[k]
            squares = renewed
    return (bridges, residuals)


def per_device(states, spans):
    sections = lax.axis_size(SECTION)
    section_index = lax.axis_index(SECTION)
    tok_count = lax.axis_size(TOK)
    layers_here, tok_rows, feature_width = states.shape
    total_rows = tok_rows * tok_count
    scaling = 1.0 / total_rows
    block_width = feature_width // sections

    def fetch(boundary):
        picked = lax.dynamic_index_in_dim(states, boundary % layers_here, 0, keepdims=False)
        return from_root(picked, SECTION, boundary // layers_here)

    def prepare(k):
        source = fetch(spans[k, 0])
        target = fetch(spans[k, 1])
        target_cols = lax.all_to_all(target, TOK, split_axis=1, concat_axis=0, tiled=True)
        sliced = lax.dynamic_slice_in_dim(source, section_index * block_width, block_width, 1)
        source_cols = lax.all_gather(sliced, TOK, axis=0, tiled=True)
        right_side = transposed(source_cols, target_cols) * scaling

        def operator(direction):
            direction_low = direction.astype(jnp.bfloat16)
            shared = sum_at_owner(
                jnp.dot(source_cols, direction_low, preferred_element_type=jnp.float32), SECTION, 0
            )
            mapped = gather_directly(shared.astype(jnp.bfloat16), SECTION, 0)
            return transposed(source_cols, mapped) * scaling + RIDGE * direction

        return (operator, right_side)

    setups = [prepare(k) for k in range(spans.shape[0])]

    def summed(values):
        totals = over_axes(jnp.stack(values), SECTION_TOK)
        return [totals[k] for k in range(len(values))]

    bridges, residuals = conjugate(
        [entry[0] for entry in setups], [entry[1] for entry in setups], summed
    )
    return (jnp.stack(bridges), jnp.stack(residuals))


def solution(mesh):
    split = Mesh(
        mesh.devices.reshape(2, 2, 4, 4, 2), ("section_0", "section_1", "tok_0", "tok_1", "tok_2")
    )
    return jax.shard_map(
        per_device,
        mesh=split,
        in_specs=(P(SECTION, TOK, None), P()),
        out_specs=(P(None, SECTION, TOK), P(None, SECTION, TOK)),
        check_vma=False,
    )
```

profile of v0, /device:TPU:1, one launch (start us, length us, event | category | flops | bytes accessed | tf_op | source)
XLA Modules:
  0.0 527.8 jit_solution(17612834347519697008)
XLA Ops:
  24.1 20.1 %reduce-scatter.5.cloned.1.call-done = bf16[16,4096]{1,0:T(8,128)(2,1)} async-done(((bf16[64,4096]{1,0:T(8,128)(2,1)}), bf16[16,4096]{1,0:T(8,128)(2,1)}) %reduce-scatter.5.cloned.1.call-update) | async-done | bytes 131088 | tf_op jit(solution)/shard_map/reduce_scatter | solution.py:28
  44.2 7.5 %all_gather.18 = bf16[64,4096]{1,0:T(8,128)(2,1)S(1)} all-gather(bf16[16,4096]{1,0:T(8,128)(2,1)} %reduce-scatter.5.cloned.1.call-done), channel_id=1, replica_groups=mesh['section_0'=2,'section_1'=2,'tok_0'=4,'tok_1'=4,'tok_2'=2] {'sectio..., dimensions={0}, use_global_device_ids=true | all-gather | bytes 655360 | tf_op jit(solution)/shard_map/all_gather | solution.py:29
  52.5 13.5 %reduce-scatter.9.cloned.1.call-done = bf16[16,4096]{1,0:T(8,128)(2,1)} async-done(((bf16[64,4096]{1,0:T(8,128)(2,1)}), bf16[16,4096]{1,0:T(8,128)(2,1)}) %reduce-scatter.9.cloned.1.call-update) | async-done | bytes 131088 | tf_op jit(solution)/shard_map/reduce_scatter | solution.py:28
  66.0 7.5 %all_gather.21 = bf16[64,4096]{1,0:T(8,128)(2,1)S(1)} all-gather(bf16[16,4096]{1,0:T(8,128)(2,1)} %reduce-scatter.9.cloned.1.call-done), channel_id=1, replica_groups=mesh['section_0'=2,'section_1'=2,'tok_0'=4,'tok_1'=4,'tok_2'=2] {'sectio..., dimensions={0}, use_global_device_ids=true | all-gather | bytes 655360 | tf_op jit(solution)/shard_map/all_gather | solution.py:29
  74.2 14.2 %reduce-scatter.7.cloned.1.call-done = bf16[16,4096]{1,0:T(8,128)(2,1)} async-done(((bf16[64,4096]{1,0:T(8,128)(2,1)}), bf16[16,4096]{1,0:T(8,128)(2,1)}) %reduce-scatter.7.cloned.1.call-update) | async-done | bytes 131088 | tf_op jit(solution)/shard_map/reduce_scatter | solution.py:28
  88.3 7.5 %all_gather.20 = bf16[64,4096]{1,0:T(8,128)(2,1)S(1)} all-gather(bf16[16,4096]{1,0:T(8,128)(2,1)} %reduce-scatter.7.cloned.1.call-done), channel_id=1, replica_groups=mesh['section_0'=2,'section_1'=2,'tok_0'=4,'tok_1'=4,'tok_2'=2] {'sectio..., dimensions={0}, use_global_device_ids=true | all-gather | bytes 655360 | tf_op jit(solution)/shard_map/all_gather | solution.py:29
  96.7 9.1 %all-to-all-start = ((bf16[64,32,128]{2,0,1:T(8,128)(2,1)}), bf16[64,32,128]{2,0,1:T(8,128)(2,1)S(1)}, u32[]{:S(2)}, u32[]{:S(2)}) async-start(bf16[64,32,128]{2,0,1:T(8,128)(2,1)} %copy_bitcast_fusion.1), calls=%async_computation.2 | async-start | bytes 1048576 | tf_op jit(solution)/shard_map/all_to_all | solution.py:106
  105.8 4.9 reduce-scatter.11.cloned.1.call-done
  110.7 7.5 %all_gather.23 = bf16[64,4096]{1,0:T(8,128)(2,1)S(1)} all-gather(bf16[16,4096]{1,0:T(8,128)(2,1)} %reduce-scatter.11.cloned.1.call-done), channel_id=1, replica_groups=mesh['section_0'=2,'section_1'=2,'tok_0'=4,'tok_1'=4,'tok_2'=2] {'sectio..., dimensions={0}, use_global_device_ids=true | all-gather | bytes 655360 | tf_op jit(solution)/shard_map/all_gather | solution.py:29
  119.9 8.4 %all-to-all-start.1 = ((bf16[64,32,128]{2,0,1:T(8,128)(2,1)}), bf16[64,32,128]{2,0,1:T(8,128)(2,1)S(1)}, u32[]{:S(2)}, u32[]{:S(2)}) async-start(bf16[64,32,128]{2,0,1:T(8,128)(2,1)} %copy_bitcast_fusion), calls=%async_computation.5 | async-start | bytes 1048576 | tf_op jit(solution)/shard_map/all_to_all | solution.py:106
  128.3 67.3 %all-gather.3.cloned.1.call-done = bf16[2048,1024]{1,0:T(8,128)(2,1)} async-done(((bf16[64,1024]{1,0:T(8,128)(2,1)}), bf16[2048,1024]{1,0:T(8,128)(2,1)}) %all-gather.3.cloned.1.call-update) | async-done | bytes 4194320 | tf_op jit(solution)/shard_map/all_gather | solution.py:108
  195.6 3.6 fusion.19
  201.5 5.2 all-to-all-start.2
  206.7 71.5 %all-gather.5.cloned.1.call-done = bf16[2048,1024]{1,0:T(8,128)(2,1)} async-done(((bf16[64,1024]{1,0:T(8,128)(2,1)}), bf16[2048,1024]{1,0:T(8,128)(2,1)}) %all-gather.5.cloned.1.call-update) | async-done | bytes 4194320 | tf_op jit(solution)/shard_map/all_gather | solution.py:108
  284.1 5.2 all-to-all-start.4
  289.4 13.4 %all-to-all-done.4 = f32[4,512,128]{2,1,0:T(8,128)S(1)} async-done(((f32[4,512,128]{2,1,0:T(8,128)}), f32[4,512,128]{2,1,0:T(8,128)S(1)}, u32[]{:S(2)}, u32[]{:S(2)}) %all-to-all-start.4) | async-done | bytes 1048608 | tf_op jit(solution)/shard_map/all_to_all | solution.py:39
  303.6 4.4 all-to-all-start.3
  308.1 7.8 %all-to-all-done.3 = bf16[4,512,128]{2,1,0:T(8,128)(2,1)S(1)} async-done(((bf16[4,512,128]{2,1,0:T(8,128)(2,1)}), bf16[4,512,128]{2,1,0:T(8,128)(2,1)S(1)}, u32[]{:S(2)}, u32[]{:S(2)}) %all-to-all-start.3) | async-done | bytes 524320 | tf_op jit(solution)/shard_map/all_to_all | solution.py:51
  316.9 4.4 all-to-all-start.5
  321.3 4.2 multiply_reduce_fusion.5
  325.5 3.6 all-to-all-done.5
  329.2 4.1 multiply_reduce_fusion.4
  335.8 3.8 all-reduce.4
  339.6 4.2 all-reduce.3
  343.8 8.1 %all-reduce.1 = (f32[2]{0:T(128)S(1)}, f32[2]{0:T(128)S(1)}) all-reduce(f32[2]{0:T(128)S(1)} %get-tuple-element.12, f32[2]{0:T(128)S(1)} %get-tuple-element.13), channel_id=1, replica_groups=mesh['section_0'=2,'section_1'=2,'tok_0'=4,'tok_1'=4,'tok_2'=2] {'tok_0'}, use_global_device_ids=true, to_apply=%region_8.9 | all-reduce | flops 4 | bytes 32 | tf_op jit(solution)/shard_map/psum | solution.py:60
  351.9 8.6 %all-reduce = (f32[2]{0:T(128)S(1)}, f32[2]{0:T(128)S(1)}) all-reduce(f32[2]{0:T(128)S(1)} %get-tuple-element.8, f32[2]{0:T(128)S(1)} %get-tuple-element.9), channel_id=1, replica_groups=mesh['section_0'=2,'section_1'=2,'tok_0'=4,'tok_1'=4,'tok_2'=2] {'tok_1'}, use_global_device_ids=true, to_apply=%region_9.10 | all-reduce | flops 4 | bytes 32 | tf_op jit(solution)/shard_map/psum | solution.py:60
  360.5 5.4 %all-reduce.2 = (f32[2]{0:T(128)S(1)}, f32[2]{0:T(128)S(1)}) all-reduce(f32[2]{0:T(128)S(1)} %get-tuple-element.6, f32[2]{0:T(128)S(1)} %get-tuple-element.7), channel_id=1, replica_groups=mesh['section_0'=2,'section_1'=2,'tok_0'=4,'tok_1'=4,'tok_2'=2] {'tok_2'}, use_global_device_ids=true, to_apply=%region_10.11 | all-reduce | flops 4 | bytes 32 | tf_op jit(solution)/shard_map/psum | solution.py:60
  372.8 3.8 psum.150
  376.6 8.8 %psum.151 = f32[2]{0:T(128)S(1)} all-reduce(f32[2]{0:T(128)S(1)} %psum.150), channel_id=1, replica_groups=mesh['section_0'=2,'section_1'=2,'tok_0'=4,'tok_1'=4,'tok_2'=2] {'sectio..., use_global_device_ids=true, to_apply=%region_23.24 | all-reduce | flops 2 | bytes 16 | tf_op jit(solution)/shard_map/psum | solution.py:60
  385.4 6.1 %psum.152 = f32[2]{0:T(128)S(1)} all-reduce(f32[2]{0:T(128)S(1)} %psum.151), channel_id=1, replica_groups=mesh['section_0'=2,'section_1'=2,'tok_0'=4,'tok_1'=4,'tok_2'=2] {'tok_0'}, use_global_device_ids=true, to_apply=%region_24.25 | all-reduce | flops 2 | bytes 16 | tf_op jit(solution)/shard_map/psum | solution.py:60
  391.4 6.0 %psum.153 = f32[2]{0:T(128)S(1)} all-reduce(f32[2]{0:T(128)S(1)} %psum.152), channel_id=1, replica_groups=mesh['section_0'=2,'section_1'=2,'tok_0'=4,'tok_1'=4,'tok_2'=2] {'tok_1'}, use_global_device_ids=true, to_apply=%region_25.26 | all-reduce | flops 2 | bytes 16 | tf_op jit(solution)/shard_map/psum | solution.py:60
  397.4 5.3 psum.154
  404.7 4.4 fusion.8
  409.1 9.1 %all-to-all-start.6 = ((f32[4,512,128]{2,1,0:T(8,128)}), f32[4,512,128]{2,1,0:T(8,128)}, u32[]{:S(2)}, u32[]{:S(2)}) async-start(f32[4,512,128]{2,1,0:T(8,128)} %bitcast.25), calls=%async_computation.10 | async-start | bytes 2097152 | tf_op jit(solution)/shard_map/all_to_all | solution.py:39
  419.7 4.4 fusion.6
  424.1 7.7 %all-to-all-done.6 = f32[4,512,128]{2,1,0:T(8,128)} async-done(((f32[4,512,128]{2,1,0:T(8,128)}), f32[4,512,128]{2,1,0:T(8,128)}, u32[]{:S(2)}, u32[]{:S(2)}) %all-to-all-start.6) | async-done | bytes 1048608 | tf_op jit(solution)/shard_map/all_to_all | solution.py:39
  431.8 5.2 all-to-all-start.8
  438.3 12.3 %all-to-all-done.8 = f32[4,512,128]{2,1,0:T(8,128)} async-done(((f32[4,512,128]{2,1,0:T(8,128)}), f32[4,512,128]{2,1,0:T(8,128)}, u32[]{:S(2)}, u32[]{:S(2)}) %all-to-all-start.8) | async-done | bytes 1048608 | tf_op jit(solution)/shard_map/all_to_all | solution.py:39
  451.4 5.1 all-to-all-start.7
  457.8 6.7 %all-to-all-done.7 = bf16[4,512,128]{2,1,0:T(8,128)(2,1)} async-done(((bf16[4,512,128]{2,1,0:T(8,128)(2,1)}), bf16[4,512,128]{2,1,0:T(8,128)(2,1)}, u32[]{:S(2)}, u32[]{:S(2)}) %all-to-all-start.7) | async-done | bytes 524320 | tf_op jit(solution)/shard_map/all_to_all | solution.py:51
  465.3 5.1 all-to-all-start.9
  470.4 5.0 multiply_reduce_fusion.1
  478.3 5.0 multiply_reduce_fusion
  484.7 3.8 psum.155
  488.4 4.2 psum.156
  492.6 7.7 %psum.157 = f32[2]{0:T(128)S(1)} all-reduce(f32[2]{0:T(128)S(1)} %psum.156), channel_id=1, replica_groups=mesh['section_0'=2,'section_1'=2,'tok_0'=4,'tok_1'=4,'tok_2'=2] {'tok_0'}, use_global_device_ids=true, to_apply=%region_33.34 | all-reduce | flops 2 | bytes 16 | tf_op jit(solution)/shard_map/psum | solution.py:60
  500.3 7.7 %psum.158 = f32[2]{0:T(128)S(1)} all-reduce(f32[2]{0:T(128)S(1)} %psum.157), channel_id=1, replica_groups=mesh['section_0'=2,'section_1'=2,'tok_0'=4,'tok_1'=4,'tok_2'=2] {'tok_1'}, use_global_device_ids=true, to_apply=%region_34.35 | all-reduce | flops 2 | bytes 16 | tf_op jit(solution)/shard_map/psum | solution.py:60
  508.0 5.3 psum.159
  (54 shorter events, 41.9 us)
Async XLA Ops:
  7.2 37.1 %reduce-scatter.5.cloned.1.call-start = ((), (), s32[]{:S(2)}) async-start(), calls=%async_computation.14 | async-start | bytes 655360 | tf_op jit(solution)/shard_map/reduce_scatter | solution.py:28
  22.0 44.0 %reduce-scatter.9.cloned.1.call-start = ((), (), s32[]{:S(2)}) async-start(), calls=%async_computation.17 | async-start | bytes 655360 | tf_op jit(solution)/shard_map/reduce_scatter | solution.py:28
  22.7 65.6 %reduce-scatter.7.cloned.1.call-start = ((), (), s32[]{:S(2)}) async-start(), calls=%async_computation.16 | async-start | bytes 655360 | tf_op jit(solution)/shard_map/reduce_scatter | solution.py:28
  23.5 87.3 %reduce-scatter.11.cloned.1.call-start = ((), (), s32[]{:S(2)}) async-start(), calls=%async_computation.19 | async-start | bytes 655360 | tf_op jit(solution)/shard_map/reduce_scatter | solution.py:28
  24.0 171.6 %all-gather.3.cloned.1.call-start = ((), (), s32[]{:S(2)}) async-start(), calls=%async_computation.15 | async-start | bytes 4325376 | tf_op jit(solution)/shard_map/all_gather | solution.py:108
  52.4 225.8 %all-gather.5.cloned.1.call-start = ((), (), s32[]{:S(2)}) async-start(), calls=%async_computation.18 | async-start | bytes 4325376 | tf_op jit(solution)/shard_map/all_gather | solution.py:108
  96.7 23.2 %all-to-all-start = ((bf16[64,32,128]{2,0,1:T(8,128)(2,1)}), bf16[64,32,128]{2,0,1:T(8,128)(2,1)S(1)}, u32[]{:S(2)}, u32[]{:S(2)}) async-start(bf16[64,32,128]{2,0,1:T(8,128)(2,1)} %copy_bitcast_fusion.1), calls=%async_computation.2 | async-start | bytes 1048576 | tf_op jit(solution)/shard_map/all_to_all | solution.py:106
  119.9 81.6 %all-to-all-start.1 = ((bf16[64,32,128]{2,0,1:T(8,128)(2,1)}), bf16[64,32,128]{2,0,1:T(8,128)(2,1)S(1)}, u32[]{:S(2)}, u32[]{:S(2)}) async-start(bf16[64,32,128]{2,0,1:T(8,128)(2,1)} %copy_bitcast_fusion), calls=%async_computation.5 | async-start | bytes 1048576 | tf_op jit(solution)/shard_map/all_to_all | solution.py:106
  195.6 3.6 copy-start
  201.5 82.6 %all-to-all-start.2 = ((f32[4,512,128]{2,1,0:T(8,128)}), f32[4,512,128]{2,1,0:T(8,128)S(1)}, u32[]{:S(2)}, u32[]{:S(2)}) async-start(f32[4,512,128]{2,1,0:T(8,128)} %bitcast.14), calls=%async_computation.6 | async-start | bytes 2097152 | tf_op jit(solution)/shard_map/all_to_all | solution.py:39
  278.2 3.6 copy-start.1
  284.1 18.7 %all-to-all-start.4 = ((f32[4,512,128]{2,1,0:T(8,128)}), f32[4,512,128]{2,1,0:T(8,128)S(1)}, u32[]{:S(2)}, u32[]{:S(2)}) async-start(f32[4,512,128]{2,1,0:T(8,128)} %bitcast.17), calls=%async_computation.8 | async-start | bytes 2097152 | tf_op jit(solution)/shard_map/all_to_all | solution.py:39
  303.6 12.3 %all-to-all-start.3 = ((bf16[4,512,128]{2,1,0:T(8,128)(2,1)}), bf16[4,512,128]{2,1,0:T(8,128)(2,1)S(1)}, u32[]{:S(2)}, u32[]{:S(2)}) async-start(bf16[4,512,128]{2,1,0:T(8,128)(2,1)} %broadcast_in_dim.12), calls=%async_computation.7 | async-start | bytes 1048576 | tf_op jit(solution)/shard_map/all_to_all | solution.py:51
  315.9 5.4 %copy-start.2 = (bf16[4,512,128]{2,1,0:T(8,128)(2,1)}, bf16[4,512,128]{2,1,0:T(8,128)(2,1)S(1)}, u32[]{:S(2)}) copy-start(bf16[4,512,128]{2,1,0:T(8,128)(2,1)S(1)} %all-to-all-done.3) | copy-start | bytes 1572868
  316.9 12.3 %all-to-all-start.5 = ((bf16[4,512,128]{2,1,0:T(8,128)(2,1)}), bf16[4,512,128]{2,1,0:T(8,128)(2,1)S(1)}, u32[]{:S(2)}, u32[]{:S(2)}) async-start(bf16[4,512,128]{2,1,0:T(8,128)(2,1)} %broadcast_in_dim.13), calls=%async_computation.9 | async-start | bytes 1048576 | tf_op jit(solution)/shard_map/all_to_all | solution.py:51
  409.1 22.7 %all-to-all-start.6 = ((f32[4,512,128]{2,1,0:T(8,128)}), f32[4,512,128]{2,1,0:T(8,128)}, u32[]{:S(2)}, u32[]{:S(2)}) async-start(f32[4,512,128]{2,1,0:T(8,128)} %bitcast.25), calls=%async_computation.10 | async-start | bytes 2097152 | tf_op jit(solution)/shard_map/all_to_all | solution.py:39
  431.8 18.8 %all-to-all-start.8 = ((f32[4,512,128]{2,1,0:T(8,128)}), f32[4,512,128]{2,1,0:T(8,128)}, u32[]{:S(2)}, u32[]{:S(2)}) async-start(f32[4,512,128]{2,1,0:T(8,128)} %bitcast.29), calls=%async_computation.12 | async-start | bytes 2097152 | tf_op jit(solution)/shard_map/all_to_all | solution.py:39
  451.4 13.0 %all-to-all-start.7 = ((bf16[4,512,128]{2,1,0:T(8,128)(2,1)}), bf16[4,512,128]{2,1,0:T(8,128)(2,1)}, u32[]{:S(2)}, u32[]{:S(2)}) async-start(bf16[4,512,128]{2,1,0:T(8,128)(2,1)} %broadcast_in_dim.14), calls=%async_computation.11 | async-start | bytes 1048576 | tf_op jit(solution)/shard_map/all_to_all | solution.py:51
  465.3 13.0 %all-to-all-start.9 = ((bf16[4,512,128]{2,1,0:T(8,128)(2,1)}), bf16[4,512,128]{2,1,0:T(8,128)(2,1)}, u32[]{:S(2)}, u32[]{:S(2)}) async-start(bf16[4,512,128]{2,1,0:T(8,128)(2,1)} %broadcast_in_dim.15), calls=%async_computation.13 | async-start | bytes 1048576 | tf_op jit(solution)/shard_map/all_to_all | solution.py:51
Sparse Core Ops, SparseCore 0:
  22.1 22.0 reduce-scatter.4
  46.6 19.3 reduce-scatter.8
  69.0 19.3 reduce-scatter.6
  90.6 20.1 reduce-scatter.10
  113.6 81.9 all-gather.2
  198.5 79.6 all-gather.4
where the time goes:
time: 534 us; the launch traced here: 528 us
  waiting for transfers between devices  249 us (47%)
  blocking collectives  119 us (22%)
  starting transfers between devices  61.4 us (11%)
  matrix products  38.9 us (7%)
  between operations  32.4 us (6%)
  other arithmetic  17.1 us (3%)
  local copies, waits for them, and re-layouts  10.8 us (2%)
    all_gather x2, waiting for transfers between devices, prepare(): source_cols = lax.all_gather(sliced, TOK, axis=0, tiled=True)  139 us
    psum x15, blocking collectives, over_axes(): value = lax.psum(value, axis)  88.7 us
    reduce_scatter x4, waiting for transfers between devices, from_root(): own = lax.psum_scatter(padded, axis, scatter_dimension=0, tiled=True)  52.7 us
    all_to_all x4, waiting for transfers between devices, sum_at_owner(): lax.all_to_all(in_blocks(value, dim, devices), axis, 0, 0, tiled=True)  33.4 us
    all_gather x4, blocking collectives, from_root(): lax.all_gather(own, axis, axis=0, tiled=True)[:len(lines)]  29.9 us
    dot_general x6, matrix products, transposed(): lax.dot_general(left, right_hand, (((0,), (0,)), ((), ())), preferred_ele...  25.5 us
    all_to_all x4, starting transfers between devices, sum_at_owner(): lax.all_to_all(in_blocks(value, dim, devices), axis, 0, 0, tiled=True)  24.7 us
    all_to_all x4, waiting for transfers between devices, copy_for_each(): return lax.all_to_all(copies, axis, split_axis=0, concat_axis=0, tiled=True)  21 us
  transfers between devices with their start and end apart: 16, of which 14 were waited for; matrix products, arithmetic and copies ran while one was open for 6% of the time, Pallas kernels for 0%

commit v1 on v0

v1 whole, which is shorter than its diff:
```python
import functools

import jax
import jax.numpy as jnp
from jax import lax
from jax.experimental import pallas as pl
from jax.experimental.pallas import tpu as pltpu
from jax.sharding import Mesh
from jax.sharding import PartitionSpec as P

MESH = pl.DeviceIdType.MESH
AXES = ("xl", "core", "y", "z", "xh")
SECTION = ("xl", "core")
TOK = ("y", "z", "xh")
RIDGE = 0.25
F32 = jnp.float32
BF16 = jnp.bfloat16


def nn(left, right):
    return jnp.dot(left, right, preferred_element_type=F32)


def nt(left, right):
    return lax.dot_general(left, right, (((1,), (1,)), ((), ())), preferred_element_type=F32)


def total(value):
    return jnp.sum(jnp.sum(value, axis=0, keepdims=True), axis=1, keepdims=True)


def kernel(
    spans,
    states,
    out_bridge,
    out_residual,
    keep_x,
    send_x,
    recv_x,
    keep_y,
    send_y,
    recv_y,
    near_x,
    near_y,
    xs,
    y_own,
    y_mid,
    ys,
    yt,
    b_t,
    ab_t,
    ar_own,
    ar_ship,
    low,
    part_out,
    part_in,
    mapped,
    ship_out,
    ship_in,
    tile_out,
    tile_in,
    sum_y,
    sum_z,
    send_sems,
    recv_sems,
):
    b = lax.axis_index("xl")
    c = lax.axis_index("core")
    y = lax.axis_index("y")
    z = lax.axis_index("z")
    h = lax.axis_index("xh")
    tokens, width = xs.shape
    scale = 1.0 / tokens
    rows = states.shape[1]
    half = rows // 2
    part = width // 2
    cols = ys.shape[-1]
    side = cols // 2

    def at(xl=b, core=c, yy=y, zz=z, xh=h):
        return (xl, core, yy, zz, xh)

    def step(value, by):
        return lax.rem(value + by, 4)

    count = [0]
    sent = []

    def message(src, dst, device):
        index = count[0]
        count[0] += 1
        copy = pltpu.make_async_remote_copy(
            src_ref=src,
            dst_ref=dst,
            send_sem=send_sems.at[index],
            recv_sem=recv_sems.at[index],
            device_id=device,
            device_id_type=MESH,
        )
        copy.start()
        sent.append(copy)
        return copy

    other = at(core=1 - c)
    partner = at(xl=1 - b)
    neighbour = at(xl=1 - b, xh=1 - h)
    opposite = at(xh=1 - h)

    barrier = pltpu.get_barrier_semaphore()
    greeted = [partner, neighbour, opposite, other]
    greeted += [at(yy=step(y, d), core=cc) for d in (1, 2, 3) for cc in (c, 1 - c)]
    greeted += [at(zz=step(z, d)) for d in (1, 2, 3)]
    for device in greeted:
        pl.semaphore_signal(barrier, inc=1, device_id=device, device_id_type=MESH)

    section = 2 * b + c

    def mine(k, which, row, count_rows, column, count_columns):
        there = spans[k, which] - 2 * section
        area = (pl.ds(row, count_rows), pl.ds(column, count_columns))
        first = states[(0, *area)]
        second = states[(1, *area)]
        zero = jnp.zeros_like(first)
        return lax.select_n(there == 0, lax.select_n(there == 1, zero, second), first)

    for k in range(2):
        for block in range(2):
            there = pl.ds(block * part, part)
            here = pl.multiple_of((2 * block + c) * part, part)
            away = pl.multiple_of((2 * block + 1 - c) * part, part)
            send_x[k, :, there] = mine(k, 0, 0, rows, away, part)
            keep_x[k, :, there] = mine(k, 0, 0, rows, here, part)
        send_y[k] = mine(k, 1, pl.multiple_of((1 - c) * half, half), half, 0, 2 * width)
        keep_y[k] = mine(k, 1, pl.multiple_of(c * half, half), half, 0, 2 * width)

    pl.semaphore_wait(barrier, len(greeted))

    pair_x = message(send_x, recv_x, other)
    pair_y = message(send_y, recv_y, other)
    pair_x.wait_recv()
    keep_x[...] = keep_x[...] + recv_x[...]
    near = [
        message(keep_x.at[1 - b], near_x.at[0], partner),
        message(keep_x.at[1 - b], near_x.at[1], neighbour),
        message(keep_x.at[b], near_x.at[2], opposite),
    ]
    pair_y.wait_recv()
    keep_y[...] = keep_y[...] + recv_y[...]
    near += [
        message(keep_y.at[1 - b], near_y.at[0], partner),
        message(keep_y.at[1 - b], near_y.at[1], neighbour),
        message(keep_y.at[b], near_y.at[2], opposite),
    ]

    def place(kind, first, second, piece=None):
        p, q = (first, second) if kind == 0 else (second, first)
        start = (kind * 16 + p * 4 + q) * rows
        if piece is None:
            return xs.at[pl.ds(start, rows)]
        return xs.at[pl.ds(start + piece * half, half)]

    def along(kind, leg, by):
        if (leg == 0) == (kind == 0):
            return at(yy=step(y, by % 4))
        return at(zz=step(z, by % 4))

    def spread(kind, first):
        return {
            by: message(
                place(kind, first, 0), place(kind, first, by % 4), along(kind, 1, by)
            )
            for by in (1, -1)
        }

    gathered = [{}, {}]

    def start(kind):
        got = gathered[kind]
        for by in (1, -1):
            got["line", by] = message(place(kind, 0, 0), place(kind, by % 4, 0), along(kind, 0, by))
        got["own"] = spread(kind, 0)

    def line(kind, by):
        got = gathered[kind]
        got["line", by].wait_recv()
        piece = 0 if by == 1 else 1
        got["far", by] = message(
            place(kind, by % 4, 0, piece), place(kind, 2, 0, piece), along(kind, 0, by)
        )
        got["spread", by % 4] = spread(kind, by % 4)

    def onward(kind, first, copies):
        got = gathered[kind]
        for by in (1, -1):
            copies[by].wait_recv()
            piece = 0 if by == 1 else 1
            got["end", first, by] = message(
                place(kind, first, by % 4, piece), place(kind, first, 2, piece), along(kind, 1, by)
            )

    def far(kind):
        got = gathered[kind]
        for by in (1, -1):
            got["far", by].wait_recv()
        got["spread", 2] = spread(kind, 2)

    near[0].wait_recv()
    xs[pl.ds(0, rows), :] = keep_x[b] + near_x[0]
    start(0)
    near[1].wait_recv()
    near[2].wait_recv()
    xs[pl.ds(16 * rows, rows), :] = near_x[1] + near_x[2]
    start(1)

    near[3].wait_recv()
    y_own[0] = keep_y[b] + near_y[0]
    near[4].wait_recv()
    near[5].wait_recv()
    y_own[1] = near_y[1] + near_y[2]
    along_y = []
    for by in (1, 3, 2):
        to = step(y, by)
        columns = pl.ds(pl.multiple_of(to * 4 * cols, 4 * cols), 4 * cols)
        along_y.append(message(y_own.at[:, :, columns], y_mid.at[:, by], at(yy=to)))
    columns = pl.ds(pl.multiple_of(y * 4 * cols, 4 * cols), 4 * cols)
    y_mid[:, 0] = y_own[:, :, columns]

    for kind in (0, 1):
        for by in (1, -1):
            line(kind, by)
    for copy in along_y:
        copy.wait_recv()
    along_z = []
    for by in (1, 3, 2):
        to = step(z, by)
        columns = pl.ds(pl.multiple_of(to * cols, cols), cols)
        along_z.append(message(y_mid.at[:, :, :, columns], ys.at[:, :, by, c], at(zz=to)))
    columns = pl.ds(pl.multiple_of(z * cols, cols), cols)
    ys[:, :, 0, c] = y_mid[:, :, :, columns]
    for kind in (0, 1):
        onward(kind, 0, gathered[kind]["own"])
    for kind in (0, 1):
        far(kind)
    for copy in along_z:
        copy.wait_recv()
    cross = message(ys.at[:, :, :, c], ys.at[:, :, :, c], other)
    for first in (1, 3, 2):
        for kind in (0, 1):
            onward(kind, first, gathered[kind]["spread", first])
    cross.wait_recv()
    yt[...] = ys[...].reshape(tokens, cols).T
    for first in (0, 1, 3, 2):
        for kind in (0, 1):
            for by in (1, -1):
                gathered[kind]["end", first, by].wait_recv()

    size = 256
    zero_row = jnp.zeros((1, size), F32)

    def right_side(j, squares):
        there = pl.ds(pl.multiple_of(j * size, size), size)
        value = nn(yt[...], xs[:, there]) * scale
        b_t[:, there] = value
        low[0, :, there] = value.astype(BF16)
        return squares + jnp.sum(value * value, axis=0, keepdims=True)

    squares = lax.fori_loop(0, width // size, right_side, zero_row)
    m0 = jnp.sum(squares, axis=1, keepdims=True)
    tile_out[0] = jnp.broadcast_to(m0, (8, 128))
    norm = message(tile_out.at[0], tile_in, other)

    def apply(turn):
        copies = []
        for i in range(tokens // size):
            value = nt(low[turn], xs[pl.ds(i * size, size), :])
            part_out[turn, i] = value.astype(BF16)
            copies.append(message(part_out.at[turn, i], part_in.at[turn, i], other))
        squares = zero_row
        for i in range(tokens // size):
            copies[i].wait_recv()
            value = part_out[turn, i].astype(F32) + part_in[turn, i].astype(F32)
            squares = squares + jnp.sum(value * value, axis=0, keepdims=True)
            mapped[:, pl.ds(i * size, size)] = value.astype(BF16)
        return jnp.sum(squares, axis=1, keepdims=True) * scale

    length = apply(0)
    norm.wait_recv()
    chip_norm = m0 + tile_in[0:1, 0:1]
    chip_curvature = length + RIDGE * chip_norm
    some = chip_curvature > 0.0
    guess = jnp.where(some, chip_norm / jnp.where(some, chip_curvature, 1.0), 1.0)

    def first_image(j, sums):
        there = pl.ds(pl.multiple_of(j * size, size), size)
        base = b_t[:, there]
        image = nn(mapped[...], xs[:, there]) * scale + RIDGE * base
        ab_t[:, there] = image
        rest = base - guess * image
        low[1, :, there] = rest.astype(BF16)
        terms = (base * image, image * image, rest * image, rest * rest)
        return tuple(s + jnp.sum(t, axis=0, keepdims=True) for s, t in zip(sums, terms))

    sums = lax.fori_loop(0, width // size, first_image, (zero_row,) * 4)
    m1, m2, cross_term, rest_norm = (jnp.sum(s, axis=1, keepdims=True) for s in sums)

    second = 0.5 * apply(1) + RIDGE * rest_norm
    m3 = (second - 2.0 * cross_term + m1) / (guess * guess)
    row = lax.broadcasted_iota(jnp.int32, (8, 128), 0)
    tile = jnp.zeros((8, 128), F32)
    for i, value in enumerate((m0, m1, m2, m3)):
        tile = jnp.where(row == i, value, tile)
    tile_out[1] = tile
    sum_y[0] = tile
    over_y = []
    for by in range(4):
        for flip in range(2):
            if by or flip:
                core = c if flip == 0 else 1 - c
                over_y.append(
                    message(tile_out.at[1], sum_y.at[2 * by + flip], at(yy=step(y, by), core=core))
                )

    def second_image(side_row, column, target):
        def body(j, _):
            there = pl.ds(pl.multiple_of(column + j * size, size), size)
            line_rows = pl.ds(pl.multiple_of(side_row, side), side)
            base = b_t[line_rows, there] - guess * ab_t[line_rows, there]
            image = nn(mapped[line_rows, :], xs[:, there]) * scale + RIDGE * base
            target[:, pl.ds(pl.multiple_of(j * size, size), size)] = image
            return 0

        lax.fori_loop(0, part // size, body, 0)

    second_image((1 - h) * side, (1 - b) * part, ar_ship)
    for copy in over_y:
        copy.wait_recv()
    tile = jnp.sum(sum_y[...], axis=0)
    tile_out[2] = tile
    sum_z[0] = tile
    over_z = [
        message(tile_out.at[2], sum_z.at[by], at(zz=step(z, by))) for by in (1, 2, 3)
    ]
    second_image(h * side, b * part, ar_own)
    for copy in over_z:
        copy.wait_recv()
    tile = jnp.sum(sum_z[...], axis=0)
    m0, m1, m2, m3 = (tile[i : i + 1, 0:1] for i in range(4))

    size1 = m0 / m1
    renewed = m0 - 2.0 * size1 * m1 + size1 * size1 * m2
    ratio = renewed / m0
    more = 1.0 + ratio
    curvature = more * more * m1 - 2.0 * more * size1 * m2 + size1 * size1 * m3
    size2 = renewed / curvature
    of_rest = size1 / guess
    of_base = more - of_rest

    def block(side_row, column):
        line_rows = pl.ds(pl.multiple_of(side_row, side), side)
        there = pl.ds(pl.multiple_of(column, part), part)
        return b_t[line_rows, there], ab_t[line_rows, there]

    def bridge_of(base, image):
        return (size1 + size2 * more) * base - (size1 * size2) * image

    def residual_of(base, image, rest_image):
        return base - (size1 + size2 * of_base) * image - (size2 * of_rest) * rest_image

    ship_out[0] = bridge_of(*block(h * side, (1 - b) * part)).astype(BF16)
    to_partner = message(ship_out.at[0], ship_in.at[0], partner)
    ship_out[1] = residual_of(*block((1 - h) * side, (1 - b) * part), ar_ship[...]).astype(BF16)
    to_neighbour = message(ship_out.at[1], ship_in.at[1], neighbour)
    base, image = block(h * side, b * part)
    out_bridge[b] = bridge_of(base, image)
    out_residual[b] = residual_of(base, image, ar_own[...])
    to_partner.wait_recv()
    out_bridge[1 - b] = ship_in[0].astype(F32)
    to_neighbour.wait_recv()
    out_residual[1 - b] = ship_in[1].astype(F32)
    for copy in sent:
        copy.wait_send()


MESSAGES = 96


def per_device(states, spans):
    _, rows, features = states.shape
    tokens = rows * 32
    width = features // 2
    cols = features // 16
    half = rows // 2
    vmem = pltpu.VMEM
    out = jax.ShapeDtypeStruct((2, cols // 2, width // 2), F32)
    bridge, residual = pl.pallas_call(
        kernel,
        out_shape=(out, out),
        in_specs=[
            pl.BlockSpec(memory_space=pltpu.SMEM),
            pl.BlockSpec(memory_space=vmem),
        ],
        out_specs=(pl.BlockSpec(memory_space=vmem), pl.BlockSpec(memory_space=vmem)),
        scratch_shapes=[
            vmem((2, rows, width), BF16),
            vmem((2, rows, width), BF16),
            vmem((2, rows, width), BF16),
            vmem((2, half, features), BF16),
            vmem((2, half, features), BF16),
            vmem((2, half, features), BF16),
            vmem((3, rows, width), BF16),
            vmem((3, half, features), BF16),
            vmem((tokens, width), BF16),
            vmem((2, half, features), BF16),
            vmem((2, 4, half, 4 * cols), BF16),
            vmem((2, 4, 4, 2, half, cols), BF16),
            vmem((cols, tokens), BF16),
            vmem((cols, width), F32),
            vmem((cols, width), F32),
            vmem((cols // 2, width // 2), F32),
            vmem((cols // 2, width // 2), F32),
            vmem((2, cols, width), BF16),
            vmem((2, tokens // 256, cols, 256), BF16),
            vmem((2, tokens // 256, cols, 256), BF16),
            vmem((cols, tokens), BF16),
            vmem((2, cols // 2, width // 2), BF16),
            vmem((2, cols // 2, width // 2), BF16),
            vmem((3, 8, 128), F32),
            vmem((8, 128), F32),
            vmem((8, 8, 128), F32),
            vmem((4, 8, 128), F32),
            pltpu.SemaphoreType.DMA((MESSAGES,)),
            pltpu.SemaphoreType.DMA((MESSAGES,)),
        ],
        compiler_params=pltpu.CompilerParams(
            collective_id=0, has_side_effects=True, vmem_limit_bytes=60 * 1024 * 1024
        ),
    )(spans, states)
    return jnp.swapaxes(bridge, 1, 2), jnp.swapaxes(residual, 1, 2)


def solution(mesh):
    split = Mesh(mesh.devices.reshape(2, 2, 4, 4, 2), AXES)
    return jax.shard_map(
        per_device,
        mesh=split,
        in_specs=(P(SECTION, TOK, None), P()),
        out_specs=(P(None, SECTION, TOK), P(None, SECTION, TOK)),
        check_vma=False,
    )
```

time: 534 us -> 119 us (0.22)
  waiting for transfers between devices: 249 us -> 0 us
  blocking collectives: 119 us -> 0 us
  Pallas kernels: 0 us -> 113 us
  starting transfers between devices: 61.4 us -> 0 us
  matrix products: 38.9 us -> 0 us
  between operations: 32.4 us -> 0.65 us
  other arithmetic: 17.1 us -> 0 us
  local copies, waits for them, and re-layouts: 10.8 us -> 3.93 us
    all_gather x2 -> x0, waiting for transfers between devices: 139 us -> none  [prepare(): source_cols = lax.all_gather(sliced, TOK, axis=0, tiled=True)]
    pallas_call x0 -> x1, Pallas kernels: none -> 113 us  [per_device(): pl.pallas_call(kernel, out_shape=(out, out), in_specs=[pl.BlockSpec(memor...]
    psum x15 -> x0, blocking collectives: 88.7 us -> none  [over_axes(): value = lax.psum(value, axis)]
    all_to_all x10 -> x0, starting transfers between devices: 61.1 us -> none  [the longest x4 24.7 us: sum_at_owner(): lax.all_to_all(in_blocks(value, dim, devices), axis, 0, 0, tiled=True)]
    all_to_all x10 -> x0, waiting for transfers between devices: 55.2 us -> none  [the longest x4 33.4 us: sum_at_owner(): lax.all_to_all(in_blocks(value, dim, devices), axis, 0, 0, tiled=True)]
    reduce_scatter x4 -> x0, waiting for transfers between devices: 52.7 us -> none  [from_root(): own = lax.psum_scatter(padded, axis, scatter_dimension=0, tiled=True)]
    dot_general x10 -> x0, matrix products: 38.9 us -> none  [the longest x6 25.5 us: transposed(): lax.dot_general(left, right_hand, (((0,), (0,)), ((), ())), preferred_ele...]
    all_gather x4 -> x0, blocking collectives: 29.9 us -> none  [from_root(): lax.all_gather(own, axis, axis=0, tiled=True)[:len(lines)]]
  transfers between devices with their start and end apart: 16 -> 0, of which waited for: 14 -> 0; matrix products, arithmetic and copies ran while one was open for 6% -> 0% of each run, Pallas kernels for 0% -> 0%
where the time goes in v1:
time: 119 us; the launch traced here: 118 us
  Pallas kernels  113 us (95%)
  local copies, waits for them, and re-layouts  3.93 us (3%)
    pallas_call x1, Pallas kernels, per_device(): pl.pallas_call(kernel, out_shape=(out, out), in_specs=[pl.BlockSpec(memor...  113 us
    unnamed x4, local copies, waits for them, and re-layouts  3.93 us

profile of v1, /device:TPU:1, one launch (start us, length us, event | category | flops | bytes accessed | tf_op | source)
XLA Modules:
  0.0 117.9 jit_solution(1422237355016268555)
XLA Ops:
  0.6 113.4 %shard_map.41 = (f32[2,128,1024]{2,1,0:T(8,128)}, f32[2,128,1024]{2,1,0:T(8,128)}) custom-call(s32[2,2]{1,0:T(2,128)} %spans.1, bf16[2,64,4096]{2,1,0:T(8,128)(2,1)} %states.1), custom_call_target="tpu_custom_call" | custom-call | tf_op jit(solution)/shard_map/pallas_call | solution.py:395
  114.0 0.0 copy-start
  114.0 2.6 %copy.4 = f32[2,1024,128]{2,1,0:T(8,128)} copy(f32[2,1024,128]{1,2,0:T(8,128)} %bitcast.3) | data formatting | bytes 2097152
  116.6 0.0 copy-done
  116.6 1.3 %copy.5 = f32[2,1024,128]{2,1,0:T(8,128)} copy(f32[2,1024,128]{1,2,0:T(8,128)S(1)} %bitcast.2) | data formatting | bytes 2097152
Async XLA Ops:
  114.0 2.6 %copy-start = (f32[2,128,1024]{2,1,0:T(8,128)S(1)}, f32[2,128,1024]{2,1,0:T(8,128)}, u32[]{:S(2)}) copy-start(f32[2,128,1024]{2,1,0:T(8,128)} %get-tuple-element.5) | copy-start | bytes 3145732

commit v2 on v1

v2 whole, which is shorter than its diff:
```python
import jax
import jax.numpy as jnp
from jax import lax
from jax.experimental import pallas as pl
from jax.experimental.pallas import tpu as pltpu
from jax.sharding import Mesh
from jax.sharding import PartitionSpec as P

MESH = pl.DeviceIdType.MESH
AXES = ("xl", "core", "y", "z", "xh")
SECTION = ("xl", "core")
TOK = ("y", "z", "xh")
RIDGE = 0.25
F32 = jnp.float32
BF16 = jnp.bfloat16


def nn(left, right):
    return jnp.dot(left, right, preferred_element_type=F32)


def kernel(
    spans,
    states,
    out_bridge,
    out_residual,
    keep_x,
    send_x,
    recv_x,
    keep_y,
    send_y,
    recv_y,
    near_x,
    near_y,
    xs,
    y_own,
    y_mid,
    ys,
    yt,
    b_t,
    ab_t,
    ar_own,
    ar_ship,
    far_b,
    far_ab,
    far_ar,
    low,
    part_out,
    part_in,
    mapped,
    tile_out,
    tile_in,
    sum_y,
    sum_z,
    sum_far,
    send_sems,
    recv_sems,
):
    b = lax.axis_index("xl")
    c = lax.axis_index("core")
    y = lax.axis_index("y")
    z = lax.axis_index("z")
    h = lax.axis_index("xh")
    tokens, width = xs.shape
    scale = 1.0 / tokens
    rows = states.shape[1]
    half = rows // 2
    part = width // 2
    cols = ys.shape[-1]
    side = cols // 2

    def at(xl=b, core=c, yy=y, zz=z, xh=h):
        return (xl, core, yy, zz, xh)

    def step(value, by):
        return lax.rem(value + by, 4)

    sent = []

    class Message:
        def __init__(self, src, dst, device):
            index = len(sent)
            self.copy = pltpu.make_async_remote_copy(
                src_ref=src,
                dst_ref=dst,
                send_sem=send_sems.at[index],
                recv_sem=recv_sems.at[index],
                device_id=device,
                device_id_type=MESH,
            )
            self.copy.start()
            self.arrived = False
            sent.append(self)

        def need(self):
            if not self.arrived:
                self.arrived = True
                self.copy.wait_recv()

    other = at(core=1 - c)
    partner = at(xl=1 - b)
    neighbour = at(xl=1 - b, xh=1 - h)
    opposite = at(xh=1 - h)

    barrier = pltpu.get_barrier_semaphore()
    greeted = [partner, neighbour, opposite, other]
    greeted += [at(yy=step(y, d), core=cc) for d in (1, 2, 3) for cc in (c, 1 - c)]
    greeted += [at(xl=xl, zz=step(z, d)) for d in (1, 2, 3) for xl in (b, 1 - b)]
    for device in greeted:
        pl.semaphore_signal(barrier, inc=1, device_id=device, device_id_type=MESH)

    section = 2 * b + c

    def mine(k, which, row, count_rows, column, count_columns):
        there = spans[k, which] - 2 * section
        area = (pl.ds(row, count_rows), pl.ds(column, count_columns))
        first = states[(0, *area)]
        second = states[(1, *area)]
        zero = jnp.zeros_like(first)
        return lax.select_n(there == 0, lax.select_n(there == 1, zero, second), first)

    for k in range(2):
        for block in range(2):
            there = pl.ds(block * part, part)
            here = pl.multiple_of((2 * block + c) * part, part)
            away = pl.multiple_of((2 * block + 1 - c) * part, part)
            send_x[k, :, there] = mine(k, 0, 0, rows, away, part)
            keep_x[k, :, there] = mine(k, 0, 0, rows, here, part)
        send_y[k] = mine(k, 1, pl.multiple_of((1 - c) * half, half), half, 0, 2 * width)
        keep_y[k] = mine(k, 1, pl.multiple_of(c * half, half), half, 0, 2 * width)

    pl.semaphore_wait(barrier, len(greeted))

    pair_far = Message(send_x.at[1 - b], recv_x.at[1 - b], other)
    pair_own = Message(send_x.at[b], recv_x.at[b], other)
    pair_y = Message(send_y, recv_y, other)
    pieces = [pl.ds(piece * half, half) for piece in range(2)]

    def ring(k, slot, device):
        return [
            Message(keep_x.at[k, piece], near_x.at[slot, piece], device) for piece in pieces
        ]

    pair_far.need()
    keep_x[1 - b] = keep_x[1 - b] + recv_x[1 - b]
    from_partner = ring(1 - b, 0, partner)
    from_neighbour = ring(1 - b, 1, neighbour)
    pair_own.need()
    keep_x[b] = keep_x[b] + recv_x[b]
    pair_y.need()
    keep_y[...] = keep_y[...] + recv_y[...]

    quarter = half // 2
    moved = {}

    def place(kind, piece, first, second, sub=None):
        p, q = (first, second) if piece == 0 else (second, first)
        row = (kind * 16 + p * 4 + q) * rows + piece * half
        if sub is None:
            return xs.at[pl.ds(row, half)]
        return xs.at[pl.ds(row + sub * quarter, quarter)]

    def along(piece, leg, by):
        if leg == piece:
            return at(yy=step(y, by % 4))
        return at(zz=step(z, by % 4))

    def spread(kind, piece, first):
        for by in (1, -1):
            moved[kind, piece, first, by] = Message(
                place(kind, piece, first, 0),
                place(kind, piece, first, by % 4),
                along(piece, 1, by),
            )

    def own(kind, piece):
        for by in (1, -1):
            moved[kind, piece, "line", by] = Message(
                place(kind, piece, 0, 0), place(kind, piece, by % 4, 0), along(piece, 0, by)
            )
        spread(kind, piece, 0)

    def line(kind, piece, by):
        moved[kind, piece, "line", by].need()
        sub = 0 if by == 1 else 1
        moved[kind, piece, "far", by] = Message(
            place(kind, piece, by % 4, 0, sub), place(kind, piece, 2, 0, sub), along(piece, 0, by)
        )
        spread(kind, piece, by % 4)

    def far(kind, piece):
        for by in (1, -1):
            moved[kind, piece, "far", by].need()
        spread(kind, piece, 2)

    def onward(kind, piece, first):
        for by in (1, -1):
            moved[kind, piece, first, by].need()
            sub = 0 if by == 1 else 1
            moved[kind, piece, first, "end", by] = Message(
                place(kind, piece, first, by % 4, sub),
                place(kind, piece, first, 2, sub),
                along(piece, 1, by),
            )

    def both(action, kind, *rest):
        for piece in range(2):
            action(kind, piece, *rest)

    def whole(kind, p):
        for by in (1, -1):
            moved[kind, 0, p, by].need()
            moved[kind, 0, p, "end", by].need()
            for first in range(4):
                if p == 2:
                    moved[kind, 1, first, "end", by].need()
                elif p == by % 4:
                    moved[kind, 1, first, by].need()

    size = 256

    def right_part(kind, p, fresh):
        whole(kind, p)
        here = pl.ds((kind * 16 + p * 4) * rows, 4 * rows)
        yt[:, here] = ys[kind, p].reshape(4 * rows, cols).T

        def body(j, _):
            there = pl.ds(pl.multiple_of(j * size, size), size)
            value = nn(yt[:, here], xs[here, there])
            b_t[:, there] = value if fresh else b_t[:, there] + value
            return 0

        lax.fori_loop(0, width // size, body, 0)

    for piece in range(2):
        from_partner[piece].need()
        xs[pieces[piece], :] = keep_x[b, pieces[piece], :] + near_x[0, pieces[piece], :]
        own(0, piece)
        if piece == 0:
            from_opposite = ring(b, 2, opposite)
    for by in (1, -1):
        both(line, 0, by)
    near_target = Message(keep_y.at[1 - b], near_y, partner)
    both(onward, 0, 0)
    for piece in range(2):
        from_neighbour[piece].need()
        from_opposite[piece].need()
        xs[pl.ds(16 * rows + piece * half, half), :] = (
            near_x[1, pieces[piece], :] + near_x[2, pieces[piece], :]
        )
        own(1, piece)
    both(far, 0)

    near_target.need()
    y_own[...] = keep_y[b] + near_y[...]
    along_y = []
    for by in (1, 3, 2):
        to = step(y, by)
        columns = pl.ds(pl.multiple_of(to * 4 * cols, 4 * cols), 4 * cols)
        along_y.append(Message(y_own.at[:, columns], y_mid.at[by], at(yy=to)))
    columns = pl.ds(pl.multiple_of(y * 4 * cols, 4 * cols), 4 * cols)
    y_mid[0] = y_own[:, columns]
    for by in (1, -1):
        both(line, 1, by)
    for first in (1, 3):
        both(onward, 0, first)
    for copy in along_y:
        copy.need()
    along_z = []
    for by in (1, 3, 2):
        to = step(z, by)
        columns = pl.ds(pl.multiple_of(to * cols, cols), cols)
        along_z.append(Message(y_mid.at[:, :, columns], ys.at[0, :, by, c], at(zz=to)))
    columns = pl.ds(pl.multiple_of(z * cols, cols), cols)
    ys[0, :, 0, c] = y_mid[:, :, columns]
    both(onward, 1, 0)
    both(far, 1)
    both(onward, 0, 2)
    for copy in along_z:
        copy.need()
    plane = Message(ys.at[0, :, :, c], ys.at[1, :, :, c], opposite)
    cross = [Message(ys.at[0, :, :, c], ys.at[0, :, :, c], other)]
    for first in (1, 3):
        both(onward, 1, first)
    plane.need()
    cross.append(Message(ys.at[1, :, :, c], ys.at[1, :, :, c], other))
    cross[0].need()
    right_part(0, 0, True)
    both(onward, 1, 2)
    right_part(0, 1, False)
    right_part(0, 3, False)
    cross[1].need()
    right_part(1, 0, False)
    right_part(1, 1, False)
    right_part(1, 3, False)

    last = []
    for kind in range(2):
        whole(kind, 2)
        here = pl.ds((kind * 16 + 8) * rows, 4 * rows)
        yt[:, here] = ys[kind, 2].reshape(4 * rows, cols).T
        last.append(here)
    zero_row = jnp.zeros((1, size), F32)

    def right_side(j, squares):
        there = pl.ds(pl.multiple_of(j * size, size), size)
        value = b_t[:, there]
        for here in last:
            value = value + nn(yt[:, here], xs[here, there])
        value = value * scale
        b_t[:, there] = value
        low[0, there, :] = value.astype(BF16).T
        return squares + jnp.sum(value * value, axis=0, keepdims=True)

    squares = lax.fori_loop(0, width // size, right_side, zero_row)
    m0 = jnp.sum(squares, axis=1, keepdims=True)
    tile_out[0] = jnp.broadcast_to(m0, (8, 128))
    norm = Message(tile_out.at[0], tile_in.at[0], other)

    shipped = (
        (partner, h * side, (1 - b) * part, 0),
        (neighbour, (1 - h) * side, (1 - b) * part + part // 2, part // 2),
    )

    def ship(source, target):
        return [
            Message(
                source.at[
                    pl.ds(pl.multiple_of(row, side), side),
                    pl.ds(pl.multiple_of(column, part // 2), part // 2),
                ],
                target.at[:, pl.ds(start, part // 2)],
                device,
            )
            for device, row, column, start in shipped
        ]

    arriving = ship(b_t, far_b)

    def apply(turn):
        copies = []
        for i in range(tokens // size):
            value = nn(xs[pl.ds(i * size, size), :], low[turn])
            part_out[turn, i] = value.astype(BF16).T
            copies.append(Message(part_out.at[turn, i], part_in.at[turn, i], other))
        squares = zero_row
        for i in range(tokens // size):
            copies[i].need()
            value = part_out[turn, i].astype(F32) + part_in[turn, i].astype(F32)
            squares = squares + jnp.sum(value * value, axis=0, keepdims=True)
            mapped[:, pl.ds(i * size, size)] = value.astype(BF16)
        return jnp.sum(squares, axis=1, keepdims=True) * scale

    length = apply(0)
    norm.need()
    chip_norm = m0 + tile_in[0, 0:1, 0:1]
    chip_curvature = length + RIDGE * chip_norm
    some = chip_curvature > 0.0
    guess = jnp.where(some, chip_norm / jnp.where(some, chip_curvature, 1.0), 1.0)

    def first_image(j, sums):
        there = pl.ds(pl.multiple_of(j * size, size), size)
        base = b_t[:, there]
        image = nn(mapped[...], xs[:, there]) * scale + RIDGE * base
        ab_t[:, there] = image
        rest = base - guess * image
        low[1, there, :] = rest.astype(BF16).T
        terms = (base * image, image * image, rest * image, rest * rest)
        return tuple(s + jnp.sum(t, axis=0, keepdims=True) for s, t in zip(sums, terms))

    sums = lax.fori_loop(0, width // size, first_image, (zero_row,) * 4)
    m1, m2, cross_term, rest_norm = (jnp.sum(s, axis=1, keepdims=True) for s in sums)

    arriving += ship(ab_t, far_ab)
    tile_out[3] = jnp.broadcast_to(guess, (8, 128))
    arriving.append(Message(tile_out.at[3], tile_in.at[1], partner))

    second = 0.5 * apply(1) + RIDGE * rest_norm
    m3 = (second - 2.0 * cross_term + m1) / (guess * guess)
    row = lax.broadcasted_iota(jnp.int32, (8, 128), 0)
    tile = jnp.zeros((8, 128), F32)
    for i, value in enumerate((m0, m1, m2, m3)):
        tile = jnp.where(row == i, value, tile)
    tile_out[1] = tile
    sum_y[0] = tile
    over_y = []
    for by in range(4):
        for flip in range(2):
            if by or flip:
                core = c if flip == 0 else 1 - c
                over_y.append(
                    Message(tile_out.at[1], sum_y.at[2 * by + flip], at(yy=step(y, by), core=core))
                )

    def second_image(side_row, column, blocks, put):
        line_rows = pl.ds(pl.multiple_of(side_row, side), side)
        for j in range(blocks):
            there = pl.ds(pl.multiple_of(column + j * size, size), size)
            base = b_t[line_rows, there] - guess * ab_t[line_rows, there]
            put(j * size, nn(mapped[line_rows, :], xs[:, there]) * scale + RIDGE * base)

    for turn, (device, row, column, start) in enumerate(shipped):

        def put(at_column, value):
            ar_ship[turn, :, at_column : at_column + size] = value.astype(BF16)

        second_image(row, column, part // 2 // size, put)
        arriving.append(
            Message(ar_ship.at[turn], far_ar.at[:, pl.ds(start, part // 2)], device)
        )
    for copy in over_y:
        copy.need()
    tile = jnp.sum(sum_y[...], axis=0)
    tile_out[2] = tile
    sum_z[0] = tile
    over_z = [Message(tile_out.at[2], sum_z.at[by], at(zz=step(z, by))) for by in (1, 2, 3)]
    over_z += [
        Message(tile_out.at[2], sum_far.at[by], at(xl=1 - b, zz=step(z, by)))
        for by in (0, 1, 2, 3)
    ]

    def put_own(at_column, value):
        ar_own[:, at_column : at_column + size] = value

    second_image(h * side, b * part, part // size, put_own)

    def finish(k, sums, guess, base, image, rest_image):
        m0, m1, m2, m3 = (sums[i : i + 1, 0:1] for i in range(4))
        size1 = m0 / m1
        renewed = m0 - 2.0 * size1 * m1 + size1 * size1 * m2
        ratio = renewed / m0
        more = 1.0 + ratio
        curvature = more * more * m1 - 2.0 * more * size1 * m2 + size1 * size1 * m3
        size2 = renewed / curvature
        of_rest = size1 / guess
        of_base = more - of_rest
        out_bridge[k] = (size1 + size2 * more) * base - (size1 * size2) * image
        out_residual[k] = (
            base - (size1 + size2 * of_base) * image - (size2 * of_rest) * rest_image
        )

    for copy in over_z:
        copy.need()
    line_rows = pl.ds(pl.multiple_of(h * side, side), side)
    there = pl.ds(pl.multiple_of(b * part, part), part)
    finish(
        b,
        jnp.sum(sum_z[...], axis=0),
        guess,
        b_t[line_rows, there],
        ab_t[line_rows, there],
        ar_own[...],
    )
    for copy in arriving:
        copy.need()
    finish(
        1 - b,
        jnp.sum(sum_far[...], axis=0),
        tile_in[1, 0:1, 0:1],
        far_b[...],
        far_ab[...],
        far_ar[...].astype(F32),
    )
    for message in sent:
        message.copy.wait_send()


MESSAGES = 144


def per_device(states, spans):
    _, rows, features = states.shape
    tokens = rows * 32
    width = features // 2
    cols = features // 16
    half = rows // 2
    vmem = pltpu.VMEM
    out = jax.ShapeDtypeStruct((2, cols // 2, width // 2), F32)
    bridge, residual = pl.pallas_call(
        kernel,
        out_shape=(out, out),
        in_specs=[
            pl.BlockSpec(memory_space=pltpu.SMEM),
            pl.BlockSpec(memory_space=vmem),
        ],
        out_specs=(pl.BlockSpec(memory_space=vmem), pl.BlockSpec(memory_space=vmem)),
        scratch_shapes=[
            vmem((2, rows, width), BF16),
            vmem((2, rows, width), BF16),
            vmem((2, rows, width), BF16),
            vmem((2, half, features), BF16),
            vmem((2, half, features), BF16),
            vmem((2, half, features), BF16),
            vmem((3, rows, width), BF16),
            vmem((half, features), BF16),
            vmem((tokens, width), BF16),
            vmem((half, features), BF16),
            vmem((4, half, 4 * cols), BF16),
            vmem((2, 4, 4, 2, half, cols), BF16),
            vmem((cols, tokens), BF16),
            vmem((cols, width), F32),
            vmem((cols, width), F32),
            vmem((cols // 2, width // 2), F32),
            vmem((2, cols // 2, width // 4), BF16),
            vmem((cols // 2, width // 2), F32),
            vmem((cols // 2, width // 2), F32),
            vmem((cols // 2, width // 2), BF16),
            vmem((2, width, cols), BF16),
            vmem((2, tokens // 256, cols, 256), BF16),
            vmem((2, tokens // 256, cols, 256), BF16),
            vmem((cols, tokens), BF16),
            vmem((4, 8, 128), F32),
            vmem((2, 8, 128), F32),
            vmem((8, 8, 128), F32),
            vmem((4, 8, 128), F32),
            vmem((4, 8, 128), F32),
            pltpu.SemaphoreType.DMA((MESSAGES,)),
            pltpu.SemaphoreType.DMA((MESSAGES,)),
        ],
        compiler_params=pltpu.CompilerParams(
            collective_id=0, has_side_effects=True, vmem_limit_bytes=44 * 1024 * 1024
        ),
    )(spans, states)
    return jnp.swapaxes(bridge, 1, 2), jnp.swapaxes(residual, 1, 2)


def solution(mesh):
    split = Mesh(mesh.devices.reshape(2, 2, 4, 4, 2), AXES)
    return jax.shard_map(
        per_device,
        mesh=split,
        in_specs=(P(SECTION, TOK, None), P()),
        out_specs=(P(None, SECTION, TOK), P(None, SECTION, TOK)),
        check_vma=False,
    )
```

time: 119 us -> 108 us (0.908); the launches traced: 118 us -> 108 us
  Pallas kernels: 113 us -> 103 us
    pallas_call x1, Pallas kernels: 113 us -> 103 us  [per_device(): pl.pallas_call(kernel, out_shape=(out, out), in_specs=[pl.BlockSpec(memor...]
    unnamed x4 -> x6, local copies, waits for them, and re-layouts: 3.93 us -> 4.51 us
where the time goes in v2:
time: 108 us
  Pallas kernels  103 us (95%)
  local copies, waits for them, and re-layouts  4.51 us (4%)
    pallas_call x1, Pallas kernels, per_device(): pl.pallas_call(kernel, out_shape=(out, out), in_specs=[pl.BlockSpec(memor...  103 us
    unnamed x6, local copies, waits for them, and re-layouts  4.51 us

profile of v2, /device:TPU:1, one launch (start us, length us, event | category | flops | bytes accessed | tf_op | source)
XLA Modules:
  0.0 108.2 jit_solution(7689755393515576040)
XLA Ops:
  0.6 0.0 copy-start
  0.6 1.2 %copy-done = bf16[2,64,4096]{2,1,0:T(8,128)(2,1)S(1)} copy-done((bf16[2,64,4096]{2,1,0:T(8,128)(2,1)S(1)}, bf16[2,64,4096]{2,1,0:T(8,128)(2,1)}, u32[]{:S(2)}) %copy-start) | copy-done | bytes 1048600
  1.9 0.0 copy-start.1
  1.9 0.7 copy-done.1
  2.5 103.1 %shard_map.41 = (f32[2,128,1024]{2,1,0:T(8,128)S(1)}, f32[2,128,1024]{2,1,0:T(8,128)S(1)}) custom-call(s32[2,2]{1,0:T(2,128)S(1)} %copy-done.1, bf16[2,64,4096]{2,1,0:T(8,128)(2,1)S(1)} %copy-done), custom_call_target="tpu_custom_call" | custom-call | tf_op jit(solution)/shard_map/pallas_call | solution.py:479
  105.6 1.3 %copy.4 = f32[2,1024,128]{2,1,0:T(8,128)} copy(f32[2,1024,128]{1,2,0:T(8,128)S(1)} %bitcast.3) | data formatting | bytes 2097152
  106.9 1.3 %copy.5 = f32[2,1024,128]{2,1,0:T(8,128)} copy(f32[2,1024,128]{1,2,0:T(8,128)S(1)} %bitcast.2) | data formatting | bytes 2097152
Async XLA Ops:
  0.6 1.2 %copy-start = (bf16[2,64,4096]{2,1,0:T(8,128)(2,1)S(1)}, bf16[2,64,4096]{2,1,0:T(8,128)(2,1)}, u32[]{:S(2)}) copy-start(bf16[2,64,4096]{2,1,0:T(8,128)(2,1)} %states.1) | copy-start | bytes 3145732
  1.9 0.7 copy-start.1

commit v3 on v2

--- a/solution.py
+++ b/solution.py
@@ -39,7 +39,7 @@
     yt,
     b_t,
     ab_t,
-    ar_own,
+    parts,
     ar_ship,
     far_b,
     far_ab,
@@ -104,7 +104,7 @@
 
     barrier = pltpu.get_barrier_semaphore()
     greeted = [partner, neighbour, opposite, other]
-    greeted += [at(yy=step(y, d), core=cc) for d in (1, 2, 3) for cc in (c, 1 - c)]
+    greeted += [at(yy=step(y, d)) for d in (1, 2, 3)]
     greeted += [at(xl=xl, zz=step(z, d)) for d in (1, 2, 3) for xl in (b, 1 - b)]
     for device in greeted:
         pl.semaphore_signal(barrier, inc=1, device_id=device, device_id_type=MESH)
@@ -203,34 +203,45 @@
                 along(piece, 1, by),
             )
 
+    def across(piece, first):
+        for by in (1, -1):
+            moved[0, piece, first, "end", by].need()
+        moved[1, piece, first, "across"] = Message(
+            place(0, piece, first, 2), place(1, piece, first, 2), opposite
+        )
+
     def both(action, kind, *rest):
         for piece in range(2):
             action(kind, piece, *rest)
 
+    def end(kind, piece, first):
+        if kind == 1 and first != 2:
+            moved[kind, piece, first, "across"].need()
+        else:
+            for by in (1, -1):
+                moved[kind, piece, first, "end", by].need()
+
     def whole(kind, p):
         for by in (1, -1):
             moved[kind, 0, p, by].need()
-            moved[kind, 0, p, "end", by].need()
-            for first in range(4):
-                if p == 2:
-                    moved[kind, 1, first, "end", by].need()
-                elif p == by % 4:
-                    moved[kind, 1, first, by].need()
+        end(kind, 0, p)
+        for first in range(4):
+            if p == 2:
+                end(kind, 1, first)
+            elif p:
+                moved[kind, 1, first, 1 if p == 1 else -1].need()
 
     size = 256
+
+    blocks = [pl.ds(j * size, size) for j in range(width // size)]
 
     def right_part(kind, p, fresh):
         whole(kind, p)
         here = pl.ds((kind * 16 + p * 4) * rows, 4 * rows)
         yt[:, here] = ys[kind, p].reshape(4 * rows, cols).T
-
-        def body(j, _):
-            there = pl.ds(pl.multiple_of(j * size, size), size)
+        for there in blocks:
             value = nn(yt[:, here], xs[here, there])
             b_t[:, there] = value if fresh else b_t[:, there] + value
-            return 0
-
-        lax.fori_loop(0, width // size, body, 0)
 
     for piece in range(2):
         from_partner[piece].need()
@@ -273,20 +284,22 @@
         along_z.append(Message(y_mid.at[:, :, columns], ys.at[0, :, by, c], at(zz=to)))
     columns = pl.ds(pl.multiple_of(z * cols, cols), cols)
     ys[0, :, 0, c] = y_mid[:, :, columns]
-    both(onward, 1, 0)
     both(far, 1)
     both(onward, 0, 2)
+    for piece in range(2):
+        across(piece, 0)
     for copy in along_z:
         copy.need()
     plane = Message(ys.at[0, :, :, c], ys.at[1, :, :, c], opposite)
     cross = [Message(ys.at[0, :, :, c], ys.at[0, :, :, c], other)]
     for first in (1, 3):
-        both(onward, 1, first)
+        for piece in range(2):
+            across(piece, first)
+    both(onward, 1, 2)
     plane.need()
     cross.append(Message(ys.at[1, :, :, c], ys.at[1, :, :, c], other))
     cross[0].need()
     right_part(0, 0, True)
-    both(onward, 1, 2)
     right_part(0, 1, False)
     right_part(0, 3, False)
     cross[1].need()
@@ -302,17 +315,15 @@
         last.append(here)
     zero_row = jnp.zeros((1, size), F32)
 
-    def right_side(j, squares):
-        there = pl.ds(pl.multiple_of(j * size, size), size)
+    squares = zero_row
+    for there in blocks:
         value = b_t[:, there]
         for here in last:
             value = value + nn(yt[:, here], xs[here, there])
         value = value * scale
         b_t[:, there] = value
         low[0, there, :] = value.astype(BF16).T
-        return squares + jnp.sum(value * value, axis=0, keepdims=True)
-
-    squares = lax.fori_loop(0, width // size, right_side, zero_row)
+        squares = squares + jnp.sum(value * value, axis=0, keepdims=True)
     m0 = jnp.sum(squares, axis=1, keepdims=True)
     tile_out[0] = jnp.broadcast_to(m0, (8, 128))
     norm = Message(tile_out.at[0], tile_in.at[0], other)
@@ -337,64 +348,86 @@
 
     arriving = ship(b_t, far_b)
 
-    def apply(turn):
+    long = tokens // 2
+    spans_of_tokens = [pl.ds(part_of * long, long) for part_of in range(2)]
+
+    def products(turn):
         copies = []
-        for i in range(tokens // size):
-            value = nn(xs[pl.ds(i * size, size), :], low[turn])
-            part_out[turn, i] = value.astype(BF16).T
-            copies.append(Message(part_out.at[turn, i], part_in.at[turn, i], other))
-        squares = zero_row
-        for i in range(tokens // size):
-            copies[i].need()
-            value = part_out[turn, i].astype(F32) + part_in[turn, i].astype(F32)
+        for part_of in range(2):
+            for i in range(long // size):
+                value = nn(xs[pl.ds(part_of * long + i * size, size), :], low[turn])
+                part_out[turn, part_of, :, pl.ds(i * size, size)] = value.astype(BF16).T
+            copies.append(
+                Message(part_out.at[turn, part_of], part_in.at[turn, part_of], other)
+            )
+        return copies
+
+    def add_up(turn, part_of, squares):
+        for i in range(long // size):
+            there = pl.ds(i * size, size)
+            value = part_out[turn, part_of, :, there].astype(F32)
+            value = value + part_in[turn, part_of, :, there].astype(F32)
             squares = squares + jnp.sum(value * value, axis=0, keepdims=True)
-            mapped[:, pl.ds(i * size, size)] = value.astype(BF16)
-        return jnp.sum(squares, axis=1, keepdims=True) * scale
-
-    length = apply(0)
+            mapped[:, pl.ds(part_of * long + i * size, size)] = value.astype(BF16)
+        return squares
+
+    row = lax.broadcasted_iota(jnp.int32, (8, 128), 0)
+
+    def tile_of(values):
+        tile = jnp.zeros((8, 128), F32)
+        for i, value in enumerate(values):
+            tile = jnp.where(row == i, value, tile)
+        return tile
+
+    copies = products(0)
+    copies[0].need()
+    squares = add_up(0, 0, zero_row)
+    for there in blocks:
+        ab_t[:, there] = nn(mapped[:, spans_of_tokens[0]], xs[spans_of_tokens[0], there])
+    copies[1].need()
+    squares = add_up(0, 1, squares)
+    length = jnp.sum(squares, axis=1, keepdims=True) * scale
     norm.need()
     chip_norm = m0 + tile_in[0, 0:1, 0:1]
     chip_curvature = length + RIDGE * chip_norm
     some = chip_curvature > 0.0
     guess = jnp.where(some, chip_norm / jnp.where(some, chip_curvature, 1.0), 1.0)
 
-    def first_image(j, sums):
-        there = pl.ds(pl.multiple_of(j * size, size), size)
+    sums = [zero_row] * 4
+    for there in blocks:
         base = b_t[:, there]
-        image = nn(mapped[...], xs[:, there]) * scale + RIDGE * base
+        image = ab_t[:, there] + nn(mapped[:, spans_of_tokens[1]], xs[spans_of_tokens[1], there])
+        image = image * scale + RIDGE * base
         ab_t[:, there] = image
         rest = base - guess * image
         low[1, there, :] = rest.astype(BF16).T
         terms = (base * image, image * image, rest * image, rest * rest)
-        return tuple(s + jnp.sum(t, axis=0, keepdims=True) for s, t in zip(sums, terms))
-
-    sums = lax.fori_loop(0, width // size, first_image, (zero_row,) * 4)
-    m1, m2, cross_term, rest_norm = (jnp.sum(s, axis=1, keepdims=True) for s in sums)
-
+        sums = [total + jnp.sum(t, axis=0, keepdims=True) for total, t in zip(sums, terms)]
+    tile = tile_of([jnp.sum(total, axis=1, keepdims=True) for total in sums])
+    tile_out[1] = tile
+    pair_sums = Message(tile_out.at[1], tile_in.at[2], other)
+
+    copies = products(1)
     arriving += ship(ab_t, far_ab)
     tile_out[3] = jnp.broadcast_to(guess, (8, 128))
     arriving.append(Message(tile_out.at[3], tile_in.at[1], partner))
-
-    second = 0.5 * apply(1) + RIDGE * rest_norm
+    pair_sums.need()
+    chip = tile + tile_in[2]
+    m1, m2, cross_term, rest_norm = (chip[i : i + 1, 0:1] for i in range(4))
+    copies[0].need()
+    squares = add_up(1, 0, zero_row)
+    copies[1].need()
+    squares = add_up(1, 1, squares)
+    second = jnp.sum(squares, axis=1, keepdims=True) * scale + RIDGE * rest_norm
     m3 = (second - 2.0 * cross_term + m1) / (guess * guess)
-    row = lax.broadcasted_iota(jnp.int32, (8, 128), 0)
-    tile = jnp.zeros((8, 128), F32)
-    for i, value in enumerate((m0, m1, m2, m3)):
-        tile = jnp.where(row == i, value, tile)
-    tile_out[1] = tile
+    tile = tile_of((chip_norm, m1, m2, m3))
+    tile_out[4] = tile
     sum_y[0] = tile
-    over_y = []
-    for by in range(4):
-        for flip in range(2):
-            if by or flip:
-                core = c if flip == 0 else 1 - c
-                over_y.append(
-                    Message(tile_out.at[1], sum_y.at[2 * by + flip], at(yy=step(y, by), core=core))
-                )
-
-    def second_image(side_row, column, blocks, put):
+    over_y = [Message(tile_out.at[4], sum_y.at[by], at(yy=step(y, by))) for by in (1, 2, 3)]
+
+    def second_image(side_row, column, count_blocks, put):
         line_rows = pl.ds(pl.multiple_of(side_row, side), side)
-        for j in range(blocks):
+        for j in range(count_blocks):
             there = pl.ds(pl.multiple_of(column + j * size, size), size)
             base = b_t[line_rows, there] - guess * ab_t[line_rows, there]
             put(j * size, nn(mapped[line_rows, :], xs[:, there]) * scale + RIDGE * base)
@@ -419,12 +452,22 @@
         for by in (0, 1, 2, 3)
     ]
 
+    line_rows = pl.ds(pl.multiple_of(h * side, side), side)
+    there = pl.ds(pl.multiple_of(b * part, part), part)
+
     def put_own(at_column, value):
-        ar_own[:, at_column : at_column + size] = value
+        parts[0, 2, pl.ds(at_column, size), :] = value.T
 
     second_image(h * side, b * part, part // size, put_own)
-
-    def finish(k, sums, guess, base, image, rest_image):
+    parts[0, 0] = b_t[line_rows, there].T
+    parts[0, 1] = ab_t[line_rows, there].T
+    for copy in arriving:
+        copy.need()
+    parts[1, 0] = far_b[...].T
+    parts[1, 1] = far_ab[...].T
+    parts[1, 2] = far_ar[...].astype(F32).T
+
+    def finish(k, sums, guess, which):
         m0, m1, m2, m3 = (sums[i : i + 1, 0:1] for i in range(4))
         size1 = m0 / m1
         renewed = m0 - 2.0 * size1 * m1 + size1 * size1 * m2
@@ -434,6 +477,7 @@
         size2 = renewed / curvature
         of_rest = size1 / guess
         of_base = more - of_rest
+        base, image, rest_image = (parts[which, i] for i in range(3))
         out_bridge[k] = (size1 + size2 * more) * base - (size1 * size2) * image
         out_residual[k] = (
             base - (size1 + size2 * of_base) * image - (size2 * of_rest) * rest_image
@@ -441,26 +485,8 @@
 
     for copy in over_z:
         copy.need()
-    line_rows = pl.ds(pl.multiple_of(h * side, side), side)
-    there = pl.ds(pl.multiple_of(b * part, part), part)
-    finish(
-        b,
-        jnp.sum(sum_z[...], axis=0),
-        guess,
-        b_t[line_rows, there],
-        ab_t[line_rows, there],
-        ar_own[...],
-    )
-    for copy in arriving:
-        copy.need()
-    finish(
-        1 - b,
-        jnp.sum(sum_far[...], axis=0),
-        tile_in[1, 0:1, 0:1],
-        far_b[...],
-        far_ab[...],
-        far_ar[...].astype(F32),
-    )
+    finish(b, jnp.sum(sum_z[...], axis=0), guess, 0)
+    finish(1 - b, jnp.sum(sum_far[...], axis=0), tile_in[1, 0:1, 0:1], 1)
     for message in sent:
         message.copy.wait_send()
 
@@ -475,8 +501,8 @@
     cols = features // 16
     half = rows // 2
     vmem = pltpu.VMEM
-    out = jax.ShapeDtypeStruct((2, cols // 2, width // 2), F32)
-    bridge, residual = pl.pallas_call(
+    out = jax.ShapeDtypeStruct((2, width // 2, cols // 2), F32)
+    return pl.pallas_call(
         kernel,
         out_shape=(out, out),
         in_specs=[
@@ -500,18 +526,18 @@
             vmem((cols, tokens), BF16),
             vmem((cols, width), F32),
             vmem((cols, width), F32),
-            vmem((cols // 2, width // 2), F32),
+            vmem((2, 3, width // 2, cols // 2), F32),
             vmem((2, cols // 2, width // 4), BF16),
             vmem((cols // 2, width // 2), F32),
             vmem((cols // 2, width // 2), F32),
             vmem((cols // 2, width // 2), BF16),
             vmem((2, width, cols), BF16),
-            vmem((2, tokens // 256, cols, 256), BF16),
-            vmem((2, tokens // 256, cols, 256), BF16),
+            vmem((2, 2, cols, tokens // 2), BF16),
+            vmem((2, 2, cols, tokens // 2), BF16),
             vmem((cols, tokens), BF16),
+            vmem((5, 8, 128), F32),
+            vmem((3, 8, 128), F32),
             vmem((4, 8, 128), F32),
-            vmem((2, 8, 128), F32),
-            vmem((8, 8, 128), F32),
             vmem((4, 8, 128), F32),
             vmem((4, 8, 128), F32),
             pltpu.SemaphoreType.DMA((MESSAGES,)),
@@ -521,7 +547,6 @@
             collective_id=0, has_side_effects=True, vmem_limit_bytes=44 * 1024 * 1024
         ),
     )(spans, states)
-    return jnp.swapaxes(bridge, 1, 2), jnp.swapaxes(residual, 1, 2)
 
 
 def solution(mesh):

time: 108 us -> 102 us (0.944)
  Pallas kernels: 103 us -> 97.7 us
    pallas_call x1, Pallas kernels: 103 us -> 97.7 us  [per_device(): pl.pallas_call(kernel, out_shape=(out, out), in_specs=[pl.BlockSpec(memor...]
where the time goes in v3:
time: 102 us
  Pallas kernels  97.7 us (96%)
  local copies, waits for them, and re-layouts  3.84 us (4%)
    pallas_call x1, Pallas kernels, per_device(): pl.pallas_call(kernel, out_shape=(out, out), in_specs=[pl.BlockSpec(memor...  97.7 us
    unnamed x6, local copies, waits for them, and re-layouts  3.84 us

profile of v3, /device:TPU:1, one launch (start us, length us, event | category | flops | bytes accessed | tf_op | source)
XLA Modules:
  0.0 102.2 jit_solution(10208902039915151462)
XLA Ops:
  0.6 0.0 copy-start
  0.6 1.2 %copy-done = bf16[2,64,4096]{2,1,0:T(8,128)(2,1)S(1)} copy-done((bf16[2,64,4096]{2,1,0:T(8,128)(2,1)S(1)}, bf16[2,64,4096]{2,1,0:T(8,128)(2,1)}, u32[]{:S(2)}) %copy-start) | copy-done | bytes 1048600
  1.9 0.0 copy-start.1
  1.9 0.7 copy-done.1
  2.5 97.7 %shard_map.41 = (f32[2,1024,128]{2,1,0:T(8,128)S(1)}, f32[2,1024,128]{2,1,0:T(8,128)S(1)}) custom-call(s32[2,2]{1,0:T(2,128)S(1)} %copy-done.1, bf16[2,64,4096]{2,1,0:T(8,128)(2,1)S(1)} %copy-done), custom_call_target="tpu_custom_call" | custom-call | tf_op jit(solution)/shard_map/pallas_call | solution.py:505
  100.2 1.0 copy.6
  101.2 1.0 copy.7
Async XLA Ops:
  0.6 1.2 %copy-start = (bf16[2,64,4096]{2,1,0:T(8,128)(2,1)S(1)}, bf16[2,64,4096]{2,1,0:T(8,128)(2,1)}, u32[]{:S(2)}) copy-start(bf16[2,64,4096]{2,1,0:T(8,128)(2,1)} %states.1) | copy-start | bytes 3145732
  1.9 0.7 copy-start.1

commit v4 on v3

--- a/solution.py
+++ b/solution.py
@@ -13,6 +13,61 @@
 RIDGE = 0.25
 F32 = jnp.float32
 BF16 = jnp.bfloat16
+
+
+ORDER = (
+    ("opposite",),
+    ("target",),
+    ("own", 0, 0),
+    ("own", 0, 1),
+    ("line", 0, 0, -1),
+    ("line", 0, 0, 1),
+    ("own", 1, 0),
+    ("line", 0, 1, -1),
+    ("own", 1, 1),
+    ("target_y",),
+    ("onward", 0, 1, 0, 1),
+    ("onward", 0, 0, 0, -1),
+    ("onward", 0, 0, 0, 1),
+    ("line", 1, 0, -1),
+    ("line", 0, 1, 1),
+    ("onward", 0, 1, 0, -1),
+    ("target_z",),
+    ("line", 1, 1, 1),
+    ("line", 1, 1, -1),
+    ("across", 0, 0),
+    ("line", 1, 0, 1),
+    ("onward", 0, 1, 3, -1),
+    ("onward", 0, 0, 1, 1),
+    ("onward", 0, 1, 3, 1),
+    ("across", 1, 0),
+    ("onward", 0, 0, 1, -1),
+    ("far", 1, 1),
+    ("far", 0, 1),
+    ("far", 0, 0),
+    ("target_plane",),
+    ("far", 1, 0),
+    ("onward", 0, 0, 3, -1),
+    ("onward", 1, 0, 3, -1),
+    ("across", 0, 1),
+    ("onward", 1, 1, 1, 1),
+    ("onward", 0, 1, 1, -1),
+    ("onward", 0, 0, 3, 1),
+    ("onward", 1, 1, 2, -1),
+    ("onward", 0, 0, 2, -1),
+    ("onward", 0, 0, 2, 1),
+    ("onward", 0, 1, 1, 1),
+    ("onward", 1, 1, 2, 1),
+    ("onward", 1, 0, 3, 1),
+    ("onward", 1, 1, 1, -1),
+    ("across", 1, 3),
+    ("onward", 0, 1, 2, 1),
+    ("target_core",),
+    ("onward", 1, 0, 2, 1),
+    ("onward", 1, 0, 2, -1),
+    ("onward", 0, 1, 2, -1),
+)
+ACROSS = tuple(step[1:] for step in ORDER if step[0] == "across")
 
 
 def nn(left, right):
@@ -174,6 +229,15 @@
             )
 
     def own(kind, piece):
+        here = pieces[piece]
+        target = pl.ds(kind * 16 * rows + piece * half, half)
+        if kind == 0:
+            from_partner[piece].need()
+            xs[target, :] = keep_x[b, here, :] + near_x[0, here, :]
+        else:
+            from_neighbour[piece].need()
+            from_opposite[piece].need()
+            xs[target, :] = near_x[1, here, :] + near_x[2, here, :]
         for by in (1, -1):
             moved[kind, piece, "line", by] = Message(
                 place(kind, piece, 0, 0), place(kind, piece, by % 4, 0), along(piece, 0, by)
@@ -193,15 +257,14 @@
             moved[kind, piece, "far", by].need()
         spread(kind, piece, 2)
 
-    def onward(kind, piece, first):
-        for by in (1, -1):
-            moved[kind, piece, first, by].need()
-            sub = 0 if by == 1 else 1
-            moved[kind, piece, first, "end", by] = Message(
-                place(kind, piece, first, by % 4, sub),
-                place(kind, piece, first, 2, sub),
-                along(piece, 1, by),
-            )
+    def onward(kind, piece, first, by):
+        moved[kind, piece, first, by].need()
+        sub = 0 if by == 1 else 1
+        moved[kind, piece, first, "end", by] = Message(
+            place(kind, piece, first, by % 4, sub),
+            place(kind, piece, first, 2, sub),
+            along(piece, 1, by),
+        )
 
     def across(piece, first):
         for by in (1, -1):
@@ -210,12 +273,8 @@
             place(0, piece, first, 2), place(1, piece, first, 2), opposite
         )
 
-    def both(action, kind, *rest):
-        for piece in range(2):
-            action(kind, piece, *rest)
-
     def end(kind, piece, first):
-        if kind == 1 and first != 2:
+        if kind == 1 and (piece, first) in ACROSS:
             moved[kind, piece, first, "across"].need()
         else:
             for by in (1, -1):
@@ -243,61 +302,60 @@
             value = nn(yt[:, here], xs[here, there])
             b_t[:, there] = value if fresh else b_t[:, there] + value
 
-    for piece in range(2):
-        from_partner[piece].need()
-        xs[pieces[piece], :] = keep_x[b, pieces[piece], :] + near_x[0, pieces[piece], :]
-        own(0, piece)
-        if piece == 0:
-            from_opposite = ring(b, 2, opposite)
-    for by in (1, -1):
-        both(line, 0, by)
-    near_target = Message(keep_y.at[1 - b], near_y, partner)
-    both(onward, 0, 0)
-    for piece in range(2):
-        from_neighbour[piece].need()
-        from_opposite[piece].need()
-        xs[pl.ds(16 * rows + piece * half, half), :] = (
-            near_x[1, pieces[piece], :] + near_x[2, pieces[piece], :]
-        )
-        own(1, piece)
-    both(far, 0)
-
-    near_target.need()
-    y_own[...] = keep_y[b] + near_y[...]
-    along_y = []
-    for by in (1, 3, 2):
-        to = step(y, by)
-        columns = pl.ds(pl.multiple_of(to * 4 * cols, 4 * cols), 4 * cols)
-        along_y.append(Message(y_own.at[:, columns], y_mid.at[by], at(yy=to)))
-    columns = pl.ds(pl.multiple_of(y * 4 * cols, 4 * cols), 4 * cols)
-    y_mid[0] = y_own[:, columns]
-    for by in (1, -1):
-        both(line, 1, by)
-    for first in (1, 3):
-        both(onward, 0, first)
-    for copy in along_y:
-        copy.need()
-    along_z = []
-    for by in (1, 3, 2):
-        to = step(z, by)
-        columns = pl.ds(pl.multiple_of(to * cols, cols), cols)
-        along_z.append(Message(y_mid.at[:, :, columns], ys.at[0, :, by, c], at(zz=to)))
-    columns = pl.ds(pl.multiple_of(z * cols, cols), cols)
-    ys[0, :, 0, c] = y_mid[:, :, columns]
-    both(far, 1)
-    both(onward, 0, 2)
-    for piece in range(2):
-        across(piece, 0)
-    for copy in along_z:
-        copy.need()
-    plane = Message(ys.at[0, :, :, c], ys.at[1, :, :, c], opposite)
-    cross = [Message(ys.at[0, :, :, c], ys.at[0, :, :, c], other)]
-    for first in (1, 3):
-        for piece in range(2):
-            across(piece, first)
-    both(onward, 1, 2)
-    plane.need()
-    cross.append(Message(ys.at[1, :, :, c], ys.at[1, :, :, c], other))
+    near_target, along_y, along_z, plane, cross = [], [], [], [], []
+    from_opposite = []
+
+    def opposite_ring():
+        from_opposite.extend(ring(b, 2, opposite))
+
+    def target():
+        near_target.append(Message(keep_y.at[1 - b], near_y, partner))
+
+    def target_y():
+        near_target[0].need()
+        y_own[...] = keep_y[b] + near_y[...]
+        for by in (1, 3, 2):
+            to = step(y, by)
+            columns = pl.ds(pl.multiple_of(to * 4 * cols, 4 * cols), 4 * cols)
+            along_y.append(Message(y_own.at[:, columns], y_mid.at[by], at(yy=to)))
+        columns = pl.ds(pl.multiple_of(y * 4 * cols, 4 * cols), 4 * cols)
+        y_mid[0] = y_own[:, columns]
+
+    def target_z():
+        for copy in along_y:
+            copy.need()
+        for by in (1, 3, 2):
+            to = step(z, by)
+            columns = pl.ds(pl.multiple_of(to * cols, cols), cols)
+            along_z.append(Message(y_mid.at[:, :, columns], ys.at[0, :, by, c], at(zz=to)))
+        columns = pl.ds(pl.multiple_of(z * cols, cols), cols)
+        ys[0, :, 0, c] = y_mid[:, :, columns]
+
+    def target_plane():
+        for copy in along_z:
+            copy.need()
+        plane.append(Message(ys.at[0, :, :, c], ys.at[1, :, :, c], opposite))
+        cross.append(Message(ys.at[0, :, :, c], ys.at[0, :, :, c], other))
+
+    def target_core():
+        plane[0].need()
+        cross.append(Message(ys.at[1, :, :, c], ys.at[1, :, :, c], other))
+
+    steps = {
+        "own": own,
+        "opposite": opposite_ring,
+        "line": line,
+        "far": far,
+        "onward": onward,
+        "across": across,
+        "target": target,
+        "target_y": target_y,
+        "target_z": target_z,
+        "target_plane": target_plane,
+        "target_core": target_core,
+    }
+    for name, *arguments in ORDER:
+        steps[name](*arguments)
     cross[0].need()
     right_part(0, 0, True)
     right_part(0, 1, False)

time: 102 us -> 89.2 us (0.87)
  Pallas kernels: 97.7 us -> 84.6 us
    pallas_call x1, Pallas kernels: 97.7 us -> 84.6 us  [per_device(): pl.pallas_call(kernel, out_shape=(out, out), in_specs=[pl.BlockSpec(memor...]
where the time goes in v4:
time: 89.2 us; the launch traced here: 89.1 us
  Pallas kernels  84.6 us (95%)
  local copies, waits for them, and re-layouts  3.84 us (4%)
    pallas_call x1, Pallas kernels, per_device(): pl.pallas_call(kernel, out_shape=(out, out), in_specs=[pl.BlockSpec(memor...  84.6 us
    unnamed x6, local copies, waits for them, and re-layouts  3.84 us

profile of v4, /device:TPU:1, one launch (start us, length us, event | category | flops | bytes accessed | tf_op | source)
XLA Modules:
  0.0 89.1 jit_solution(9462517237166372133)
XLA Ops:
  0.6 0.0 copy-start
  0.6 1.2 %copy-done = bf16[2,64,4096]{2,1,0:T(8,128)(2,1)S(1)} copy-done((bf16[2,64,4096]{2,1,0:T(8,128)(2,1)S(1)}, bf16[2,64,4096]{2,1,0:T(8,128)(2,1)}, u32[]{:S(2)}) %copy-start) | copy-done | bytes 1048600
  1.9 0.0 copy-start.1
  1.9 0.7 copy-done.1
  2.5 84.6 %shard_map.41 = (f32[2,1024,128]{2,1,0:T(8,128)S(1)}, f32[2,1024,128]{2,1,0:T(8,128)S(1)}) custom-call(s32[2,2]{1,0:T(2,128)S(1)} %copy-done.1, bf16[2,64,4096]{2,1,0:T(8,128)(2,1)S(1)} %copy-done), custom_call_target="tpu_custom_call" | custom-call | tf_op jit(solution)/shard_map/pallas_call | solution.py:563
  87.1 1.0 %copy.6 = f32[2,1024,128]{2,1,0:T(8,128)} copy(f32[2,1024,128]{2,1,0:T(8,128)S(1)} %get-tuple-element.4) | data formatting | bytes 2097152
  88.1 1.0 %copy.7 = f32[2,1024,128]{2,1,0:T(8,128)} copy(f32[2,1024,128]{2,1,0:T(8,128)S(1)} %get-tuple-element.5) | data formatting | bytes 2097152
Async XLA Ops:
  0.6 1.2 %copy-start = (bf16[2,64,4096]{2,1,0:T(8,128)(2,1)S(1)}, bf16[2,64,4096]{2,1,0:T(8,128)(2,1)}, u32[]{:S(2)}) copy-start(bf16[2,64,4096]{2,1,0:T(8,128)(2,1)} %states.1) | copy-start | bytes 3145732
  1.9 0.7 copy-start.1

commit v5 on v4

--- a/solution.py
+++ b/solution.py
@@ -76,9 +76,10 @@
 
 def kernel(
     spans,
-    states,
+    states_hbm,
     out_bridge,
     out_residual,
+    states,
     keep_x,
     send_x,
     recv_x,
@@ -110,7 +111,10 @@
     sum_far,
     send_sems,
     recv_sems,
+    load_sem,
 ):
+    load = pltpu.make_async_copy(states_hbm, states, load_sem)
+    load.start()
     b = lax.axis_index("xl")
     c = lax.axis_index("core")
     y = lax.axis_index("y")
@@ -164,6 +168,8 @@
     for device in greeted:
         pl.semaphore_signal(barrier, inc=1, device_id=device, device_id_type=MESH)
 
+    load.wait()
+
     section = 2 * b + c
 
     def mine(k, which, row, count_rows, column, count_columns):
@@ -186,26 +192,35 @@
 
     pl.semaphore_wait(barrier, len(greeted))
 
-    pair_far = Message(send_x.at[1 - b], recv_x.at[1 - b], other)
+    quarter = half // 2
+    first_rows, later_rows = pl.ds(0, quarter), pl.ds(quarter, rows - quarter)
+    pair_far = [
+        Message(send_x.at[1 - b, there], recv_x.at[1 - b, there], other)
+        for there in (first_rows, later_rows)
+    ]
     pair_own = Message(send_x.at[b], recv_x.at[b], other)
     pair_y = Message(send_y, recv_y, other)
     pieces = [pl.ds(piece * half, half) for piece in range(2)]
 
-    def ring(k, slot, device):
+    quarters = [pl.ds(i * quarter, quarter) for i in range(4)]
+
+    def ring(k, slot, device, parts_of):
         return [
-            Message(keep_x.at[k, piece], near_x.at[slot, piece], device) for piece in pieces
+            Message(keep_x.at[k, there], near_x.at[slot, there], device) for there in parts_of
         ]
 
-    pair_far.need()
-    keep_x[1 - b] = keep_x[1 - b] + recv_x[1 - b]
-    from_partner = ring(1 - b, 0, partner)
-    from_neighbour = ring(1 - b, 1, neighbour)
+    from_partner = []
+    for copy, there in zip(pair_far, (first_rows, later_rows)):
+        copy.need()
+        keep_x[1 - b, there] = keep_x[1 - b, there] + recv_x[1 - b, there]
+        sent_now = quarters[:1] if there is first_rows else quarters[1:]
+        from_partner += ring(1 - b, 0, partner, sent_now)
+    from_neighbour = ring(1 - b, 1, neighbour, pieces)
     pair_own.need()
     keep_x[b] = keep_x[b] + recv_x[b]
     pair_y.need()
     keep_y[...] = keep_y[...] + recv_y[...]
 
-    quarter = half // 2
     moved = {}
 
     def place(kind, piece, first, second, sub=None):
@@ -228,21 +243,44 @@
                 along(piece, 1, by),
             )
 
+    class Both:
+        def __init__(self, *messages):
+            self.messages = messages
+
+        def need(self):
+            for message in self.messages:
+                message.need()
+
+    def own_part(kind, piece, sub):
+        copies = {}
+        for leg in (0, 1):
+            for by in (1, -1):
+                target = (by % 4, 0) if leg == 0 else (0, by % 4)
+                copies[leg, by] = Message(
+                    place(kind, piece, 0, 0, sub),
+                    place(kind, piece, *target, sub),
+                    along(piece, leg, by),
+                )
+        return copies
+
     def own(kind, piece):
-        here = pieces[piece]
-        target = pl.ds(kind * 16 * rows + piece * half, half)
         if kind == 0:
-            from_partner[piece].need()
-            xs[target, :] = keep_x[b, here, :] + near_x[0, here, :]
+            copies = []
+            for sub in range(2):
+                there = quarters[2 * piece + sub]
+                from_partner[2 * piece + sub].need()
+                xs[there, :] = keep_x[b, there, :] + near_x[0, there, :]
+                copies.append(own_part(kind, piece, sub))
+            copies = {key: Both(copies[0][key], copies[1][key]) for key in copies[0]}
         else:
+            here = pieces[piece]
             from_neighbour[piece].need()
             from_opposite[piece].need()
-            xs[target, :] = near_x[1, here, :] + near_x[2, here, :]
+            xs[pl.ds(16 * rows + piece * half, half), :] = near_x[1, here, :] + near_x[2, here, :]
+            copies = own_part(kind, piece, None)
         for by in (1, -1):
-            moved[kind, piece, "line", by] = Message(
-                place(kind, piece, 0, 0), place(kind, piece, by % 4, 0), along(piece, 0, by)
-            )
-        spread(kind, piece, 0)
+            moved[kind, piece, "line", by] = copies[0, by]
+            moved[kind, piece, 0, by] = copies[1, by]
 
     def line(kind, piece, by):
         moved[kind, piece, "line", by].need()
@@ -306,7 +344,7 @@
     from_opposite = []
 
     def opposite_ring():
-        from_opposite.extend(ring(b, 2, opposite))
+        from_opposite.extend(ring(b, 2, opposite, pieces))
 
     def target():
         near_target.append(Message(keep_y.at[1 - b], near_y, partner))
@@ -406,12 +444,12 @@
 
     arriving = ship(b_t, far_b)
 
-    long = tokens // 2
-    spans_of_tokens = [pl.ds(part_of * long, long) for part_of in range(2)]
+    long = tokens // 4
+    token_halves = [pl.ds(i * 2 * long, 2 * long) for i in range(2)]
 
     def products(turn):
         copies = []
-        for part_of in range(2):
+        for part_of in range(4):
             for i in range(long // size):
                 value = nn(xs[pl.ds(part_of * long + i * size, size), :], low[turn])
                 part_out[turn, part_of, :, pl.ds(i * size, size)] = value.astype(BF16).T
@@ -421,6 +459,7 @@
         return copies
 
     def add_up(turn, part_of, squares):
+        copies[part_of].need()
         for i in range(long // size):
             there = pl.ds(i * size, size)
             value = part_out[turn, part_of, :, there].astype(F32)
@@ -438,12 +477,10 @@
         return tile
 
     copies = products(0)
-    copies[0].need()
-    squares = add_up(0, 0, zero_row)
+    squares = add_up(0, 1, add_up(0, 0, zero_row))
     for there in blocks:
-        ab_t[:, there] = nn(mapped[:, spans_of_tokens[0]], xs[spans_of_tokens[0], there])
-    copies[1].need()
-    squares = add_up(0, 1, squares)
+        ab_t[:, there] = nn(mapped[:, token_halves[0]], xs[token_halves[0], there])
+    squares = add_up(0, 3, add_up(0, 2, squares))
     length = jnp.sum(squares, axis=1, keepdims=True) * scale
     norm.need()
     chip_norm = m0 + tile_in[0, 0:1, 0:1]
@@ -454,7 +491,7 @@
     sums = [zero_row] * 4
     for there in blocks:
         base = b_t[:, there]
-        image = ab_t[:, there] + nn(mapped[:, spans_of_tokens[1]], xs[spans_of_tokens[1], there])
+        image = ab_t[:, there] + nn(mapped[:, token_halves[1]], xs[token_halves[1], there])
         image = image * scale + RIDGE * base
         ab_t[:, there] = image
         rest = base - guess * image
@@ -472,10 +509,9 @@
     pair_sums.need()
     chip = tile + tile_in[2]
     m1, m2, cross_term, rest_norm = (chip[i : i + 1, 0:1] for i in range(4))
-    copies[0].need()
-    squares = add_up(1, 0, zero_row)
-    copies[1].need()
-    squares = add_up(1, 1, squares)
+    squares = zero_row
+    for part_of in range(4):
+        squares = add_up(1, part_of, squares)
     second = jnp.sum(squares, axis=1, keepdims=True) * scale + RIDGE * rest_norm
     m3 = (second - 2.0 * cross_term + m1) / (guess * guess)
     tile = tile_of((chip_norm, m1, m2, m3))
@@ -549,7 +585,7 @@
         message.copy.wait_send()
 
 
-MESSAGES = 144
+MESSAGES = 168
 
 
 def per_device(states, spans):
@@ -565,10 +601,11 @@
         out_shape=(out, out),
         in_specs=[
             pl.BlockSpec(memory_space=pltpu.SMEM),
-            pl.BlockSpec(memory_space=vmem),
+            pl.BlockSpec(memory_space=pltpu.HBM),
         ],
         out_specs=(pl.BlockSpec(memory_space=vmem), pl.BlockSpec(memory_space=vmem)),
         scratch_shapes=[
+            vmem((2, rows, features), BF16),
             vmem((2, rows, width), BF16),
             vmem((2, rows, width), BF16),
             vmem((2, rows, width), BF16),
@@ -590,8 +627,8 @@
             vmem((cols // 2, width // 2), F32),
             vmem((cols // 2, width // 2), BF16),
             vmem((2, width, cols), BF16),
-            vmem((2, 2, cols, tokens // 2), BF16),
-            vmem((2, 2, cols, tokens // 2), BF16),
+            vmem((2, 4, cols, tokens // 4), BF16),
+            vmem((2, 4, cols, tokens // 4), BF16),
             vmem((cols, tokens), BF16),
             vmem((5, 8, 128), F32),
             vmem((3, 8, 128), F32),
@@ -600,9 +637,10 @@
             vmem((4, 8, 128), F32),
             pltpu.SemaphoreType.DMA((MESSAGES,)),
             pltpu.SemaphoreType.DMA((MESSAGES,)),
+            pltpu.SemaphoreType.DMA,
         ],
         compiler_params=pltpu.CompilerParams(
-            collective_id=0, has_side_effects=True, vmem_limit_bytes=44 * 1024 * 1024
+            collective_id=0, has_side_effects=True, vmem_limit_bytes=51 * 1024 * 1024
         ),
     )(spans, states)
 

time: 89.2 us -> 87 us (0.975)
  local copies, waits for them, and re-layouts: 3.84 us -> 2.61 us
  Pallas kernels: 84.6 us -> 83.6 us
    unnamed x6 -> x4, local copies, waits for them, and re-layouts: 3.84 us -> 2.61 us
    pallas_call x1, Pallas kernels: 84.6 us -> 83.6 us  [per_device(): pl.pallas_call(kernel, out_shape=(out, out), in_specs=[pl.BlockSpec(memor...]
where the time goes in v5:
time: 87 us; the launch traced here: 86.8 us
  Pallas kernels  83.6 us (96%)
  local copies, waits for them, and re-layouts  2.61 us (3%)
    pallas_call x1, Pallas kernels, per_device(): pl.pallas_call(kernel, out_shape=(out, out), in_specs=[pl.BlockSpec(memor...  83.6 us
    unnamed x4, local copies, waits for them, and re-layouts  2.61 us

profile of v5, /device:TPU:1, one launch (start us, length us, event | category | flops | bytes accessed | tf_op | source)
XLA Modules:
  0.0 86.8 jit_solution(9945161730570955554)
XLA Ops:
  0.6 0.0 copy-start
  0.6 0.7 copy-done
  1.3 83.6 %shard_map.41 = (f32[2,1024,128]{2,1,0:T(8,128)S(1)}, f32[2,1024,128]{2,1,0:T(8,128)S(1)}) custom-call(s32[2,2]{1,0:T(2,128)S(1)} %copy-done, bf16[2,64,4096]{2,1,0:T(8,128)(2,1)} %states_hbm.1), custom_call_target="tpu_custom_call" | custom-call | tf_op jit(solution)/shard_map/pallas_call | solution.py:599
  84.9 1.0 %copy.6 = f32[2,1024,128]{2,1,0:T(8,128)} copy(f32[2,1024,128]{2,1,0:T(8,128)S(1)} %get-tuple-element.4) | data formatting | bytes 2097152
  85.9 1.0 %copy.7 = f32[2,1024,128]{2,1,0:T(8,128)} copy(f32[2,1024,128]{2,1,0:T(8,128)S(1)} %get-tuple-element.5) | data formatting | bytes 2097152
Async XLA Ops:
  0.6 0.7 copy-start

commit v6 on v5

--- a/solution.py
+++ b/solution.py
@@ -502,8 +502,8 @@
     tile_out[1] = tile
     pair_sums = Message(tile_out.at[1], tile_in.at[2], other)
 
+    arriving += ship(ab_t, far_ab)
     copies = products(1)
-    arriving += ship(ab_t, far_ab)
     tile_out[3] = jnp.broadcast_to(guess, (8, 128))
     arriving.append(Message(tile_out.at[3], tile_in.at[1], partner))
     pair_sums.need()
@@ -526,13 +526,14 @@
             base = b_t[line_rows, there] - guess * ab_t[line_rows, there]
             put(j * size, nn(mapped[line_rows, :], xs[:, there]) * scale + RIDGE * base)
 
+    arriving_rest = []
     for turn, (device, row, column, start) in enumerate(shipped):
 
         def put(at_column, value):
             ar_ship[turn, :, at_column : at_column + size] = value.astype(BF16)
 
         second_image(row, column, part // 2 // size, put)
-        arriving.append(
+        arriving_rest.append(
             Message(ar_ship.at[turn], far_ar.at[:, pl.ds(start, part // 2)], device)
         )
     for copy in over_y:
@@ -559,7 +560,6 @@
         copy.need()
     parts[1, 0] = far_b[...].T
     parts[1, 1] = far_ab[...].T
-    parts[1, 2] = far_ar[...].astype(F32).T
 
     def finish(k, sums, guess, which):
         m0, m1, m2, m3 = (sums[i : i + 1, 0:1] for i in range(4))
@@ -577,9 +577,14 @@
             base - (size1 + size2 * of_base) * image - (size2 * of_rest) * rest_image
         )
 
-    for copy in over_z:
+    for copy in over_z[:3]:
         copy.need()
     finish(b, jnp.sum(sum_z[...], axis=0), guess, 0)
+    for copy in arriving_rest:
+        copy.need()
+    parts[1, 2] = far_ar[...].astype(F32).T
+    for copy in over_z[3:]:
+        copy.need()
     finish(1 - b, jnp.sum(sum_far[...], axis=0), tile_in[1, 0:1, 0:1], 1)
     for message in sent:
         message.copy.wait_send()

time: 87 us -> 83.8 us (0.963)
  Pallas kernels: 83.6 us -> 80.3 us
    pallas_call x1, Pallas kernels: 83.6 us -> 80.3 us  [per_device(): pl.pallas_call(kernel, out_shape=(out, out), in_specs=[pl.BlockSpec(memor...]
where the time goes in v6:
time: 83.8 us; the launch traced here: 83.6 us
  Pallas kernels  80.3 us (96%)
  local copies, waits for them, and re-layouts  2.61 us (3%)
    pallas_call x1, Pallas kernels, per_device(): pl.pallas_call(kernel, out_shape=(out, out), in_specs=[pl.BlockSpec(memor...  80.3 us
    unnamed x4, local copies, waits for them, and re-layouts  2.61 us

profile of v6, /device:TPU:1, one launch (start us, length us, event | category | flops | bytes accessed | tf_op | source)
XLA Modules:
  0.0 83.6 jit_solution(17984603490948708491)
XLA Ops:
  0.6 0.0 copy-start
  0.6 0.7 copy-done
  1.3 80.3 %shard_map.41 = (f32[2,1024,128]{2,1,0:T(8,128)S(1)}, f32[2,1024,128]{2,1,0:T(8,128)S(1)}) custom-call(s32[2,2]{1,0:T(2,128)S(1)} %copy-done, bf16[2,64,4096]{2,1,0:T(8,128)(2,1)} %states_hbm.1), custom_call_target="tpu_custom_call" | custom-call | tf_op jit(solution)/shard_map/pallas_call | solution.py:604
  81.6 1.0 %copy.6 = f32[2,1024,128]{2,1,0:T(8,128)} copy(f32[2,1024,128]{2,1,0:T(8,128)S(1)} %get-tuple-element.4) | data formatting | bytes 2097152
  82.6 1.0 %copy.7 = f32[2,1024,128]{2,1,0:T(8,128)} copy(f32[2,1024,128]{2,1,0:T(8,128)S(1)} %get-tuple-element.5) | data formatting | bytes 2097152
Async XLA Ops:
  0.6 0.7 copy-start

commit v7 on v6

--- a/solution.py
+++ b/solution.py
@@ -16,56 +16,54 @@
 
 
 ORDER = (
-    ("opposite",),
+    ("own", 0, 0),
     ("target",),
-    ("own", 0, 0),
     ("own", 0, 1),
+    ("onward", 0, 0, 0, -1),
     ("line", 0, 0, -1),
     ("line", 0, 0, 1),
+    ("line", 0, 1, -1),
+    ("onward", 0, 1, 0, 1),
+    ("opposite",),
+    ("target_y",),
+    ("onward", 0, 0, 3, 1),
+    ("onward", 0, 1, 0, -1),
+    ("onward", 0, 0, 0, 1),
+    ("onward", 0, 0, 3, -1),
+    ("line", 0, 1, 1),
     ("own", 1, 0),
-    ("line", 0, 1, -1),
     ("own", 1, 1),
-    ("target_y",),
-    ("onward", 0, 1, 0, 1),
-    ("onward", 0, 0, 0, -1),
-    ("onward", 0, 0, 0, 1),
+    ("across", 0, 0),
+    ("across", 0, 3),
+    ("onward", 0, 0, 1, 1),
+    ("onward", 0, 0, 1, -1),
+    ("onward", 0, 1, 3, -1),
+    ("across", 1, 0),
+    ("onward", 0, 1, 3, 1),
+    ("target_z",),
+    ("line", 1, 1, -1),
+    ("far", 0, 0),
+    ("line", 1, 1, 1),
+    ("line", 1, 0, 1),
     ("line", 1, 0, -1),
-    ("line", 0, 1, 1),
-    ("onward", 0, 1, 0, -1),
-    ("target_z",),
-    ("line", 1, 1, 1),
-    ("line", 1, 1, -1),
-    ("across", 0, 0),
-    ("line", 1, 0, 1),
-    ("onward", 0, 1, 3, -1),
-    ("onward", 0, 0, 1, 1),
-    ("onward", 0, 1, 3, 1),
-    ("across", 1, 0),
-    ("onward", 0, 0, 1, -1),
+    ("across", 0, 1),
+    ("onward", 0, 1, 1, -1),
+    ("across", 1, 3),
+    ("far", 0, 1),
+    ("onward", 0, 1, 1, 1),
     ("far", 1, 1),
-    ("far", 0, 1),
-    ("far", 0, 0),
     ("target_plane",),
     ("far", 1, 0),
-    ("onward", 0, 0, 3, -1),
-    ("onward", 1, 0, 3, -1),
-    ("across", 0, 1),
-    ("onward", 1, 1, 1, 1),
-    ("onward", 0, 1, 1, -1),
-    ("onward", 0, 0, 3, 1),
+    ("onward", 0, 0, 2, 1),
+    ("onward", 0, 1, 2, -1),
+    ("across", 1, 1),
+    ("onward", 0, 0, 2, -1),
+    ("onward", 0, 1, 2, 1),
+    ("onward", 1, 0, 2, -1),
     ("onward", 1, 1, 2, -1),
-    ("onward", 0, 0, 2, -1),
-    ("onward", 0, 0, 2, 1),
-    ("onward", 0, 1, 1, 1),
+    ("onward", 1, 0, 2, 1),
     ("onward", 1, 1, 2, 1),
-    ("onward", 1, 0, 3, 1),
-    ("onward", 1, 1, 1, -1),
-    ("across", 1, 3),
-    ("onward", 0, 1, 2, 1),
     ("target_core",),
-    ("onward", 1, 0, 2, 1),
-    ("onward", 1, 0, 2, -1),
-    ("onward", 0, 1, 2, -1),
 )
 ACROSS = tuple(step[1:] for step in ORDER if step[0] == "across")
 
@@ -111,10 +109,8 @@
     sum_far,
     send_sems,
     recv_sems,
-    load_sem,
+    load_sems,
 ):
-    load = pltpu.make_async_copy(states_hbm, states, load_sem)
-    load.start()
     b = lax.axis_index("xl")
     c = lax.axis_index("core")
     y = lax.axis_index("y")
@@ -124,6 +120,14 @@
     scale = 1.0 / tokens
     rows = states.shape[1]
     half = rows // 2
+    quarter = half // 2
+    first_rows, later_rows = pl.ds(0, quarter), pl.ds(quarter, rows - quarter)
+    loads = [
+        pltpu.make_async_copy(states_hbm.at[:, there], states.at[:, there], load_sems.at[i])
+        for i, there in enumerate((first_rows, later_rows))
+    ]
+    for load in loads:
+        load.start()
     part = width // 2
     cols = ys.shape[-1]
     side = cols // 2
@@ -168,8 +172,6 @@
     for device in greeted:
         pl.semaphore_signal(barrier, inc=1, device_id=device, device_id_type=MESH)
 
-    load.wait()
-
     section = 2 * b + c
 
     def mine(k, which, row, count_rows, column, count_columns):
@@ -180,28 +182,29 @@
         zero = jnp.zeros_like(first)
         return lax.select_n(there == 0, lax.select_n(there == 1, zero, second), first)
 
-    for k in range(2):
+    def fill(k, row, count_rows):
         for block in range(2):
-            there = pl.ds(block * part, part)
+            area = (k, pl.ds(row, count_rows), pl.ds(block * part, part))
             here = pl.multiple_of((2 * block + c) * part, part)
             away = pl.multiple_of((2 * block + 1 - c) * part, part)
-            send_x[k, :, there] = mine(k, 0, 0, rows, away, part)
-            keep_x[k, :, there] = mine(k, 0, 0, rows, here, part)
+            send_x[area] = mine(k, 0, row, count_rows, away, part)
+            keep_x[area] = mine(k, 0, row, count_rows, here, part)
+
+    pieces = [pl.ds(piece * half, half) for piece in range(2)]
+    loads[0].wait()
+    fill(1 - b, 0, quarter)
+    pl.semaphore_wait(barrier, len(greeted))
+
+    pair_far = [Message(send_x.at[1 - b, first_rows], recv_x.at[1 - b, first_rows], other)]
+    loads[1].wait()
+    fill(1 - b, quarter, rows - quarter)
+    pair_far.append(Message(send_x.at[1 - b, later_rows], recv_x.at[1 - b, later_rows], other))
+    fill(b, 0, rows)
+    pair_own = Message(send_x.at[b], recv_x.at[b], other)
+    for k in range(2):
         send_y[k] = mine(k, 1, pl.multiple_of((1 - c) * half, half), half, 0, 2 * width)
         keep_y[k] = mine(k, 1, pl.multiple_of(c * half, half), half, 0, 2 * width)
-
-    pl.semaphore_wait(barrier, len(greeted))
-
-    quarter = half // 2
-    first_rows, later_rows = pl.ds(0, quarter), pl.ds(quarter, rows - quarter)
-    pair_far = [
-        Message(send_x.at[1 - b, there], recv_x.at[1 - b, there], other)
-        for there in (first_rows, later_rows)
-    ]
-    pair_own = Message(send_x.at[b], recv_x.at[b], other)
     pair_y = Message(send_y, recv_y, other)
-    pieces = [pl.ds(piece * half, half) for piece in range(2)]
-
     quarters = [pl.ds(i * quarter, quarter) for i in range(4)]
 
     def ring(k, slot, device, parts_of):
@@ -642,7 +645,7 @@
             vmem((4, 8, 128), F32),
             pltpu.SemaphoreType.DMA((MESSAGES,)),
             pltpu.SemaphoreType.DMA((MESSAGES,)),
-            pltpu.SemaphoreType.DMA,
+            pltpu.SemaphoreType.DMA((2,)),
         ],
         compiler_params=pltpu.CompilerParams(
             collective_id=0, has_side_effects=True, vmem_limit_bytes=51 * 1024 * 1024

time: 83.8 us -> 83.6 us (level)
  no operation moved by 1% of the time
where the time goes in v7:
time: 83.6 us; the launch traced here: 83.5 us
  Pallas kernels  80.2 us (96%)
  local copies, waits for them, and re-layouts  2.61 us (3%)
    pallas_call x1, Pallas kernels, per_device(): pl.pallas_call(kernel, out_shape=(out, out), in_specs=[pl.BlockSpec(memor...  80.2 us
    unnamed x4, local copies, waits for them, and re-layouts  2.61 us

profile of v7, /device:TPU:1, one launch (start us, length us, event | category | flops | bytes accessed | tf_op | source)
XLA Modules:
  0.0 83.5 jit_solution(10417322518915086839)
XLA Ops:
  0.6 0.0 copy-start
  0.6 0.7 copy-done
  1.3 80.2 %shard_map.41 = (f32[2,1024,128]{2,1,0:T(8,128)S(1)}, f32[2,1024,128]{2,1,0:T(8,128)S(1)}) custom-call(s32[2,2]{1,0:T(2,128)S(1)} %copy-done, bf16[2,64,4096]{2,1,0:T(8,128)(2,1)} %states_hbm.1), custom_call_target="tpu_custom_call" | custom-call | tf_op jit(solution)/shard_map/pallas_call | solution.py:607
  81.5 1.0 %copy.6 = f32[2,1024,128]{2,1,0:T(8,128)} copy(f32[2,1024,128]{2,1,0:T(8,128)S(1)} %get-tuple-element.4) | data formatting | bytes 2097152
  82.5 1.0 %copy.7 = f32[2,1024,128]{2,1,0:T(8,128)} copy(f32[2,1024,128]{2,1,0:T(8,128)S(1)} %get-tuple-element.5) | data formatting | bytes 2097152
Async XLA Ops:
  0.6 0.7 copy-start

commit v8 on v7

--- a/solution.py
+++ b/solution.py
@@ -55,10 +55,13 @@
     ("target_plane",),
     ("far", 1, 0),
     ("onward", 0, 0, 2, 1),
+    ("right", 0, 0, True),
     ("onward", 0, 1, 2, -1),
     ("across", 1, 1),
     ("onward", 0, 0, 2, -1),
     ("onward", 0, 1, 2, 1),
+    ("right", 0, 1, False),
+    ("right", 0, 3, False),
     ("onward", 1, 0, 2, -1),
     ("onward", 1, 1, 2, -1),
     ("onward", 1, 0, 2, 1),
@@ -336,6 +339,7 @@
     blocks = [pl.ds(j * size, size) for j in range(width // size)]
 
     def right_part(kind, p, fresh):
+        cross[kind].need()
         whole(kind, p)
         here = pl.ds((kind * 16 + p * 4) * rows, 4 * rows)
         yt[:, here] = ys[kind, p].reshape(4 * rows, cols).T
@@ -394,14 +398,10 @@
         "target_z": target_z,
         "target_plane": target_plane,
         "target_core": target_core,
+        "right": right_part,
     }
     for name, *arguments in ORDER:
         steps[name](*arguments)
-    cross[0].need()
-    right_part(0, 0, True)
-    right_part(0, 1, False)
-    right_part(0, 3, False)
-    cross[1].need()
     right_part(1, 0, False)
     right_part(1, 1, False)
     right_part(1, 3, False)

time: 83.6 us -> 83.6 us (level)
  no operation moved by 1% of the time
where the time goes in v8:
time: 83.6 us; the launch traced here: 83.5 us
  Pallas kernels  80.2 us (96%)
  local copies, waits for them, and re-layouts  2.61 us (3%)
    pallas_call x1, Pallas kernels, per_device(): pl.pallas_call(kernel, out_shape=(out, out), in_specs=[pl.BlockSpec(memor...  80.2 us
    unnamed x4, local copies, waits for them, and re-layouts  2.61 us

profile of v8, /device:TPU:1, one launch (start us, length us, event | category | flops | bytes accessed | tf_op | source)
XLA Modules:
  0.0 83.5 jit_solution(4443570237310286026)
XLA Ops:
  0.6 0.0 copy-start
  0.6 0.7 copy-done
  1.3 80.2 %shard_map.41 = (f32[2,1024,128]{2,1,0:T(8,128)S(1)}, f32[2,1024,128]{2,1,0:T(8,128)S(1)}) custom-call(s32[2,2]{1,0:T(2,128)S(1)} %copy-done, bf16[2,64,4096]{2,1,0:T(8,128)(2,1)} %states_hbm.1), custom_call_target="tpu_custom_call" | custom-call | tf_op jit(solution)/shard_map/pallas_call | solution.py:607
  81.5 1.0 %copy.6 = f32[2,1024,128]{2,1,0:T(8,128)} copy(f32[2,1024,128]{2,1,0:T(8,128)S(1)} %get-tuple-element.4) | data formatting | bytes 2097152
  82.5 1.0 %copy.7 = f32[2,1024,128]{2,1,0:T(8,128)} copy(f32[2,1024,128]{2,1,0:T(8,128)S(1)} %get-tuple-element.5) | data formatting | bytes 2097152
Async XLA Ops:
  0.6 0.7 copy-start
